TPU v7x, 32 devices: a whole 2x2x4 slice. The times are simulated.
32 devices in a mesh: frame: 8 (over z, x), row: 4 (over y, core).
Axes of the slice: x: 2, y: 2, z: 4, core: 2. Of those that a mesh axis runs over, the one named last changes fastest.
Arguments:
- clip: bfloat16 [16, 16, 256, 128], P('frame', 'row'), may hold values from -6 to 6
- first_kernel: bfloat16 [3, 3, 3, 128, 128], replicated, may hold values from -0.109375 to 0.109375
- second_kernel: bfloat16 [3, 3, 3, 128, 128], replicated, may hold values from -0.109375 to 0.109375
- cotangent: bfloat16 [16, 16, 256, 128], P('frame', 'row'), may hold values from -6 to 6
Outputs:
- critic_map: bfloat16 [16, 16, 256, 128], P('frame', 'row')
- clip_grad: bfloat16 [16, 16, 256, 128], P('frame', 'row')
- first_grad: float32 [3, 3, 3, 128, 128], replicated
- second_grad: float32 [3, 3, 3, 128, 128], replicated
All inputs are finite; a program needn't handle non-finite values.
Results may differ from a plain program's by a relative error of at most 0.012.
Values may be sent and summed in bfloat16 or wider, within the bound.
No kernel may reach another device: no remote copies, remote signals or barrier semaphores. Data moves between devices by JAX's collectives and lax.ppermute only.
A program may use at most 64 MiB of HBM per device.

v0:
```python
import jax
import jax.numpy as jnp
from jax import lax
from jax.experimental import pallas as pl
from jax.experimental.pallas import tpu as pltpu
from jax.sharding import PartitionSpec as P

TAPS = 3
BF = jnp.bfloat16
F32 = jnp.float32


def shifted(rows):
    n, width, ch = rows.shape
    flat = rows.reshape(n * width, ch).astype(F32)
    col = lax.broadcasted_iota(jnp.int32, (n, width, ch), 1)
    before = pltpu.roll(flat, 1, 0).reshape(n, width, ch)
    after = pltpu.roll(flat, n * width - 1, 0).reshape(n, width, ch)
    before = jnp.where(col == 0, 0.0, before).astype(BF)
    after = jnp.where(col == width - 1, 0.0, after).astype(BF)
    return before, rows, after


def fill(win, own, other, own_first):
    ch = own[0].shape[-1]
    frames, height = own[0].shape[:2]
    first = (0, frames) if own_first else (2, 0)
    for start, (body, top, bottom), count in ((first[0], own, frames), (first[1], other, 2)):
        for f in range(count):
            for ref, row, size in ((top, 0, 1), (body, 1, height), (bottom, height + 1, 1)):
                for c, part in enumerate(shifted(ref[f])):
                    win[start + f, row : row + size, :, c * ch : (c + 1) * ch] = part


def window_product(win, weights, frames, height):
    width = win.shape[2]
    taps = [(f, b) for f in range(frames + 2) for b in range(TAPS)]
    acc = None
    for n in range(0, len(taps), 2):
        group = taps[n : n + 2]
        lhs = [win[f, b : b + height].reshape(height * width, win.shape[3]) for f, b in group]
        rhs = weights[n : n + len(group)].reshape(-1, weights.shape[2])
        lhs = jnp.concatenate(lhs, axis=1) if len(lhs) > 1 else lhs[0]
        part = jnp.dot(lhs, rhs, preferred_element_type=F32)
        acc = part if acc is None else acc + part
    return acc


def call(body, outs, scratch, *args):
    return pl.pallas_call(
        body,
        out_shape=outs,
        scratch_shapes=scratch,
        compiler_params=pltpu.CompilerParams(vmem_limit_bytes=56 << 20),
    )(*args)


def prepare(first_kernel, second_kernel, frames):
    ch = first_kernel.shape[-1]
    shape = ((frames + 2) * TAPS, TAPS * ch, frames * ch)

    def body(k1, k2, *outs):
        for kernel, ahead, back in ((k1, outs[0], outs[1]), (k2, outs[2], outs[3])):
            ahead[...] = jnp.zeros(shape, BF)
            back[...] = jnp.zeros(shape, BF)
            for a in range(TAPS):
                for b in range(TAPS):
                    for c in range(TAPS):
                        w = kernel[a, b, c]
                        wt = w.astype(F32).T.astype(BF)
                        a2, b2, c2 = TAPS - 1 - a, TAPS - 1 - b, TAPS - 1 - c
                        for t in range(frames):
                            o = slice(t * ch, (t + 1) * ch)
                            ahead[(t + a) * TAPS + b, c * ch : (c + 1) * ch, o] = w
                            back[(t + a2) * TAPS + b2, c2 * ch : (c2 + 1) * ch, o] = wt

    return call(body, [jax.ShapeDtypeStruct(shape, BF)] * 4, [], first_kernel, second_kernel)


def window_scratch(shape):
    frames, height, width, ch = shape
    return pltpu.VMEM((frames + 2, height + 2, width, TAPS * ch), BF)


def sigmoid(z):
    return 1.0 / (1.0 + jnp.exp(-z))


def first_layer(own, other, weights):
    shape = own[0].shape
    frames, height, width, ch = shape

    def body(x, xt, xb, y, yt, yb, w, act, slope, win):
        fill(win, (x, xt, xb), (y, yt, yb), False)
        acc = window_product(win, w, frames, height)
        s = sigmoid(acc)
        a = (acc * s).astype(BF)
        d = s * (1.0 + acc * (1.0 - s))
        for t in range(frames):
            o = slice(t * ch, (t + 1) * ch)
            act[t] = a[:, o].reshape(height, width, ch)
            slope[t] = d[:, o].reshape(height, width, ch)

    outs = [jax.ShapeDtypeStruct(shape, BF), jax.ShapeDtypeStruct(shape, F32)]
    return call(body, outs, [window_scratch(shape)], *own, *other, weights)


def second_layer(own, other, weights, cotangent):
    shape = own[0].shape
    frames, height, width, ch = shape

    def body(x, xt, xb, y, yt, yb, w, cot, out, delta, win):
        fill(win, (x, xt, xb), (y, yt, yb), False)
        acc = window_product(win, w, frames, height)
        s = sigmoid(acc)
        a = (acc * s).astype(BF)
        d = s * (1.0 + acc * (1.0 - s))
        for t in range(frames):
            o = slice(t * ch, (t + 1) * ch)
            out[t] = a[:, o].reshape(height, width, ch)
            delta[t] = (cot[t].astype(F32) * d[:, o].reshape(height, width, ch)).astype(BF)

    outs = [jax.ShapeDtypeStruct(shape, BF)] * 2
    return call(body, outs, [window_scratch(shape)], *own, *other, weights, cotangent)


def input_grad(own, other, weights, slope=None):
    shape = own[0].shape
    frames, height, width, ch = shape

    def body(x, xt, xb, y, yt, yb, w, *rest):
        out, win = rest[-2:]
        fill(win, (x, xt, xb), (y, yt, yb), True)
        acc = window_product(win, w, frames, height)
        for t in range(frames):
            part = acc[:, t * ch : (t + 1) * ch].reshape(height, width, ch)
            if slope is not None:
                part = part * rest[0][t]
            out[t] = part.astype(BF)

    extra = () if slope is None else (slope,)
    return call(body, jax.ShapeDtypeStruct(shape, BF), [window_scratch(shape)], *own, *other, weights, *extra)


def weight_grad(own, other, delta, scale, chunks, padded):
    shape = own[0].shape
    frames, height, width, ch = shape
    per_chunk = TAPS**3 * ch // chunks

    def body(x, xt, xb, y, yt, yb, d, out, win, sums):
        fill(win, (x, xt, xb), (y, yt, yb), False)
        if padded > per_chunk:
            out[:, per_chunk:] = jnp.zeros((chunks, padded - per_chunk, ch), BF)
        wide = jnp.concatenate([d[t].reshape(height * width, ch) for t in range(frames)], axis=1)
        turned = wide.T
        for f in range(frames + 2):
            rhs = [win[f, b : b + height].reshape(height * width, TAPS * ch) for b in range(TAPS)]
            part = jnp.dot(turned, jnp.concatenate(rhs, axis=1), preferred_element_type=F32)
            for t in range(frames):
                a = f - t
                if 0 <= a < TAPS:
                    mine = part[t * ch : (t + 1) * ch]
                    sums[a] = mine if t == 0 else sums[a] + mine
        for n in range(TAPS**3):
            a, bc = divmod(n, TAPS * TAPS)
            block = (sums[a, :, bc * ch : (bc + 1) * ch].T * scale).astype(BF)
            row = n * ch
            while row < (n + 1) * ch:
                chunk, at = divmod(row, per_chunk)
                size = min((n + 1) * ch - row, per_chunk - at)
                out[chunk, at : at + size] = block[row - n * ch : row - n * ch + size]
                row += size

    scratch = [window_scratch(shape), pltpu.VMEM((TAPS, ch, TAPS * TAPS * ch), F32)]
    out = jax.ShapeDtypeStruct((chunks, padded, ch), BF)
    return call(body, out, scratch, *own, *other, delta)


def exchanged(value, step):
    frames, rows = lax.axis_size("frame"), lax.axis_size("row")
    near = value[-2:] if step > 0 else value[:2]
    top, bottom = value[:, :1], value[:, -1:]
    near_top, near_bottom = near[:, :1], near[:, -1:]
    along = [(i, i + step) for i in range(frames) if 0 <= i + step < frames]
    both = ("frame", "row")
    other = lax.ppermute(near, "frame", along)
    down = [(i * rows + j, k * rows + j + 1) for i, k in along for j in range(rows - 1)]
    up = [(i * rows + j + 1, k * rows + j) for i, k in along for j in range(rows - 1)]
    other_top = lax.ppermute(near_bottom, both, down)
    other_bottom = lax.ppermute(near_top, both, up)
    own_top = lax.ppermute(bottom, "row", [(j, j + 1) for j in range(rows - 1)])
    own_bottom = lax.ppermute(top, "row", [(j + 1, j) for j in range(rows - 1)])
    return (value, own_top, own_bottom), (other, other_top, other_bottom)


def bits(axis):
    size = lax.axis_size(axis)
    return [(axis, n) for n in range(size.bit_length() - 1)]


def reduced(value):
    ch = value.shape[-1]
    order = bits("row") + bits("frame")
    part = value.reshape(-1, ch)
    for axis, n in order:
        mine = (lax.axis_index(axis) >> n) & 1
        halves = part.reshape(2, -1, ch)
        sent = lax.dynamic_index_in_dim(halves, 1 - mine, 0, False).astype(BF)
        kept = lax.dynamic_index_in_dim(halves, mine, 0, False).astype(F32)
        pairs = [(i, i ^ (1 << n)) for i in range(lax.axis_size(axis))]
        part = kept + lax.ppermute(sent, axis, pairs).astype(F32)
    part = part.astype(BF)
    for axis, n in reversed(order):
        mine = (lax.axis_index(axis) >> n) & 1
        pairs = [(i, i ^ (1 << n)) for i in range(lax.axis_size(axis))]
        got = lax.ppermute(part, axis, pairs)
        part = jnp.where(mine == 0, jnp.concatenate([part, got]), jnp.concatenate([got, part]))
    return part.reshape(value.shape)


def on_device(clip, first_kernel, second_kernel, cotangent):
    frames, height, width, ch = clip.shape
    n_frame, n_row = lax.axis_size("frame"), lax.axis_size("row")
    grad_scale = 1.0 / float(frames * n_frame * height * n_row * width) ** 0.5
    rows = TAPS**3 * ch // n_row
    unit = 16 * n_frame
    padded = -(-rows // unit) * unit

    def finish(grad):
        return reduced(grad)[:, :rows].astype(F32).reshape(TAPS, TAPS, TAPS, ch, ch)

    clip_near = exchanged(clip, 1)
    first_ahead, first_back, second_ahead, second_back = prepare(first_kernel, second_kernel, frames)
    act, slope = first_layer(*clip_near, first_ahead)
    act_near = exchanged(act, 1)
    critic_map, second_delta = second_layer(*act_near, second_ahead, cotangent)
    second_near = exchanged(second_delta, -1)
    second_grad = finish(weight_grad(*act_near, second_delta, grad_scale, n_row, padded))
    first_delta = input_grad(*second_near, second_back, slope)
    first_near = exchanged(first_delta, -1)
    first_grad = finish(weight_grad(*clip_near, first_delta, grad_scale, n_row, padded))
    clip_grad = input_grad(*first_near, first_back)
    return critic_map, clip_grad, first_grad, second_grad


def solution(mesh):
    placed = (P("frame", "row", None, None), P(), P(), P("frame", "row", None, None))
    return jax.shard_map(
        on_device,
        mesh=mesh,
        in_specs=placed,
        out_specs=(P("frame", "row", None, None), P("frame", "row", None, None), P(), P()),
        check_vma=False,
    )
```

profile of v0, /device:TPU:0, one launch (start us, length us, event | category | flops | bytes accessed | tf_op | source)
XLA Modules:
  0.0 179.3 jit_solution(4280702196864895561)
XLA Ops:
  0.6 4.9 %collective-permute-start.2 = (bf16[2,4,256,128]{3,2,1,0:T(8,128)(2,1)}, bf16[2,4,256,128]{3,2,1,0:T(8,128)(2,1)S(1)}, u32[]{:S(2)}, u32[]{:S(2)}) collective-permute-start(bf16[2,4,256,128]{3,2,1,0:T(8,128)(2,1)} %x.3), channel_id=1, source_target_pairs={{0,4},{4,8},{8,12},{12,16},{16,20},{20,24},{24,28},{1,5},{5,9},{9,... | collective-permute-start | bytes 1572872 | tf_op jit(solution)/shard_map/ppermute | solution.py:186
  5.5 1.0 fusion.13
  6.5 1.5 collective-permute-start
  8.0 1.3 collective-permute-start.1
  9.3 5.7 %collective-permute-start.3 = (bf16[2,1,256,128]{3,2,1,0:T(8,128)(2,1)S(1)}, bf16[2,1,256,128]{3,2,1,0:T(8,128)(2,1)S(1)}, u32[]{:S(2)}, u32[]{:S(2)}) collective-permute-start(bf16[2,1,256,128]{3,2,1,0:T(8,128)(2,1)S(1)} %get-tuple-element.27), channel_id=1, source_target_pairs={{0,5},{1,6},{2,7},{4,9},{5,10},{6,11},{8,13},{9,14},{10,15},{12,17... | collective-permute-start | bytes 393224 | tf_op jit(solution)/shard_map/ppermute | solution.py:189
  15.1 0.7 collective-permute-start.4
  15.7 6.0 %shard_map.75 = (bf16[12,384,256]{2,1,0:T(8,128)(2,1)}, bf16[12,384,256]{2,1,0:T(8,128)(2,1)}, bf16[12,384,256]{2,1,0:T(8,128)(2,1)}, bf16[12,384,256]{2,1,0:T(8,128)(2,1)}) custom-call(bf16[3,3,3,128,128]{4,3,2,1,0:T(8,128)(2,1)} %k1.1, bf16[3,3,3,128,128]{4,3,2,1,0:T(8,128)(2,1)} %k2.1), custom_call_target="tpu_custom_call" | custom-call | tf_op jit(solution)/shard_map/pallas_call | solution.py:50
  22.8 6.2 %shard_map.76 = (bf16[2,4,256,128]{3,2,1,0:T(8,128)(2,1)}, f32[2,4,256,128]{3,2,1,0:T(8,128)}) custom-call(bf16[2,4,256,128]{3,2,1,0:T(8,128)(2,1)} %x.3, bf16[2,1,256,128]{3,2,1,0:T(8,128)(2,1)} %copy-done.6, bf16[2,1,256,128]{3,2,1,0:T(8,128)(2,1)} %copy-done.7, bf16[2,4,256,128]{3,2,1,0:T(8,128)(2,1)} %copy-done.3, bf16[2,1,256,128]{3,2,1,0:T(8,128)(2,1)} %copy-done.8, ...), custom_call_target="tpu_custom_call" | custom-call | tf_op jit(solution)/shard_map/pallas_call | solution.py:50
  28.9 4.0 %collective-permute-start.7 = (bf16[2,4,256,128]{3,2,1,0:T(8,128)(2,1)}, bf16[2,4,256,128]{3,2,1,0:T(8,128)(2,1)S(1)}, u32[]{:S(2)}, u32[]{:S(2)}) collective-permute-start(bf16[2,4,256,128]{3,2,1,0:T(8,128)(2,1)} %get-tuple-element.13.x), channel_id=1, source_target_pairs={{0,4},{4,8},{8,12},{12,16},{16,20},{20,24},{24,28},{1,5},{5,9},{9,... | collective-permute-start | bytes 1572872 | tf_op jit(solution)/shard_map/ppermute | solution.py:186
  33.0 1.0 fusion.12
  34.0 3.9 %collective-permute-start.5 = (bf16[2,1,256,128]{3,2,1,0:T(8,128)(2,1)S(1)}, bf16[2,1,256,128]{3,2,1,0:T(8,128)(2,1)S(1)}, u32[]{:S(2)}, u32[]{:S(2)}) collective-permute-start(bf16[2,1,256,128]{3,2,1,0:T(8,128)(2,1)S(1)} %get-tuple-element.25), channel_id=1, source_target_pairs={{0,1},{1,2},{2,3},{4,5},{5,6},{6,7},{8,9},{9,10},{10,11},{12,13},{... | collective-permute-start | bytes 393224 | tf_op jit(solution)/shard_map/ppermute | solution.py:191
  37.9 1.3 collective-permute-start.6
  39.2 6.5 %collective-permute-start.8 = (bf16[2,1,256,128]{3,2,1,0:T(8,128)(2,1)S(1)}, bf16[2,1,256,128]{3,2,1,0:T(8,128)(2,1)S(1)}, u32[]{:S(2)}, u32[]{:S(2)}) collective-permute-start(bf16[2,1,256,128]{3,2,1,0:T(8,128)(2,1)S(1)} %get-tuple-element.25), channel_id=1, source_target_pairs={{0,5},{1,6},{2,7},{4,9},{5,10},{6,11},{8,13},{9,14},{10,15},{12,17... | collective-permute-start | bytes 393224 | tf_op jit(solution)/shard_map/ppermute | solution.py:189
  45.7 0.7 collective-permute-start.9
  46.4 2.3 %collective-permute-done.8.yt = bf16[2,1,256,128]{3,2,1,0:T(8,128)(2,1)S(1)} collective-permute-done((bf16[2,1,256,128]{3,2,1,0:T(8,128)(2,1)S(1)}, bf16[2,1,256,128]{3,2,1,0:T(8,128)(2,1)S(1)}, u32[]{:S(2)}, u32[]{:S(2)}) %collective-permute-start.8) | collective-permute-done | bytes 131104 | tf_op jit(solution)/shard_map/ppermute | solution.py:189
  49.7 6.2 %shard_map.77 = (bf16[2,4,256,128]{3,2,1,0:T(8,128)(2,1)}, bf16[2,4,256,128]{3,2,1,0:T(8,128)(2,1)}) custom-call(bf16[2,4,256,128]{3,2,1,0:T(8,128)(2,1)} %get-tuple-element.13.x, bf16[2,1,256,128]{3,2,1,0:T(8,128)(2,1)} %copy-done.10, bf16[2,1,256,128]{3,2,1,0:T(8,128)(2,1)} %copy-done.11, bf16[2,4,256,128]{3,2,1,0:T(8,128)(2,1)} %copy-done.4, ...), custom_call_target="tpu_custom_call" | custom-call | tf_op jit(solution)/shard_map/pallas_call | solution.py:50
  55.9 5.6 %shard_map.81 = bf16[4,896,128]{2,1,0:T(8,128)(2,1)} custom-call(bf16[2,4,256,128]{3,2,1,0:T(8,128)(2,1)} %get-tuple-element.13.x, bf16[2,1,256,128]{3,2,1,0:T(8,128)(2,1)} %copy-done.10, bf16[2,1,256,128]{3,2,1,0:T(8,128)(2,1)} %copy-done.11, bf16[2,4,256,128]{3,2,1,0:T(8,128)(2,1)} %copy-done.4, bf16[2,1,256,128]{3,2,1,0:T(8,128)(2,1)} %copy-done.12, ...), custom_call_target="tpu_custom_call" | custom-call | tf_op jit(solution)/shard_map/pallas_call | solution.py:50
  61.4 1.0 dynamic-slice_bitcast_fusion
  62.5 2.5 %collective-permute-start.30 = (bf16[1792,128]{1,0:T(8,128)(2,1)S(1)}, bf16[1792,128]{1,0:T(8,128)(2,1)S(1)}, u32[]{:S(2)}, u32[]{:S(2)}) collective-permute-start(bf16[1792,128]{1,0:T(8,128)(2,1)S(1)} %dynamic-slice_bitcast_fusion), channel_id=1, source_target_pairs={{0,1},{1,0},{2,3},{3,2},{4,5},{5,4},{6,7},{7,6},{8,9},{9,8},{10,11... | collective-permute-start | bytes 1376264 | tf_op jit(solution)/shard_map/ppermute | solution.py:211
  65.1 1.9 %collective-permute-start.10 = (bf16[2,1,256,128]{3,2,1,0:T(8,128)(2,1)S(1)}, bf16[2,1,256,128]{3,2,1,0:T(8,128)(2,1)S(1)}, u32[]{:S(2)}, u32[]{:S(2)}) collective-permute-start(bf16[2,1,256,128]{3,2,1,0:T(8,128)(2,1)S(1)} %get-tuple-element.23), channel_id=1, source_target_pairs={{0,1},{1,2},{2,3},{4,5},{5,6},{6,7},{8,9},{9,10},{10,11},{12,13},{... | collective-permute-start | bytes 393224 | tf_op jit(solution)/shard_map/ppermute | solution.py:191
  67.0 0.7 collective-permute-start.13
  67.7 1.3 collective-permute-start.11
  69.0 1.3 collective-permute-start.14
  70.3 1.5 collective-permute-start.12
  71.8 1.1 convert_add_fusion
  73.0 6.1 %collective-permute-start.31 = (bf16[896,128]{1,0:T(8,128)(2,1)S(1)}, bf16[896,128]{1,0:T(8,128)(2,1)S(1)}, u32[]{:S(2)}, u32[]{:S(2)}) collective-permute-start(bf16[896,128]{1,0:T(8,128)(2,1)S(1)} %fusion.1), channel_id=1, source_target_pairs={{0,2},{1,3},{2,0},{3,1},{4,6},{5,7},{6,4},{7,5},{8,10},{9,11},{10,... | collective-permute-start | bytes 688136 | tf_op jit(solution)/shard_map/ppermute | solution.py:211
  79.1 1.8 collective-permute-done.14.yb
  80.9 10.2 %collective-permute-done.12.y = bf16[2,4,256,128]{3,2,1,0:T(8,128)(2,1)S(1)} collective-permute-done((bf16[2,4,256,128]{3,2,1,0:T(8,128)(2,1)S(1)}, bf16[2,4,256,128]{3,2,1,0:T(8,128)(2,1)S(1)}, u32[]{:S(2)}, u32[]{:S(2)}) %collective-permute-start.12) | collective-permute-done | bytes 524320 | tf_op jit(solution)/shard_map/ppermute | solution.py:186
  91.1 0.8 copy-done.14
  91.8 5.9 %shard_map.78.x.d = bf16[2,4,256,128]{3,2,1,0:T(8,128)(2,1)} custom-call(bf16[2,4,256,128]{3,2,1,0:T(8,128)(2,1)} %get-tuple-element.16.x.d, bf16[2,1,256,128]{3,2,1,0:T(8,128)(2,1)} %copy-done.17, bf16[2,1,256,128]{3,2,1,0:T(8,128)(2,1)} %copy-done.19, bf16[2,4,256,128]{3,2,1,0:T(8,128)(2,1)} %copy-done.14, bf16[2,1,256,128]{3,2,1,0:T(8,128)(2,1)} %copy-done.18, ...), custom_call_target="tpu_custom_call" | custom-call | tf_op jit(solution)/shard_map/pallas_call | solution.py:50
  97.7 5.5 %shard_map.80 = bf16[4,896,128]{2,1,0:T(8,128)(2,1)} custom-call(bf16[2,4,256,128]{3,2,1,0:T(8,128)(2,1)} %x.3, bf16[2,1,256,128]{3,2,1,0:T(8,128)(2,1)} %copy-done.6, bf16[2,1,256,128]{3,2,1,0:T(8,128)(2,1)} %copy-done.7, bf16[2,4,256,128]{3,2,1,0:T(8,128)(2,1)} %copy-done.3, bf16[2,1,256,128]{3,2,1,0:T(8,128)(2,1)} %copy-done.8, ...), custom_call_target="tpu_custom_call" | custom-call | tf_op jit(solution)/shard_map/pallas_call | solution.py:50
  103.2 1.1 dynamic-slice_bitcast_fusion.1
  104.9 2.6 %collective-permute-start.32 = (bf16[448,128]{1,0:T(8,128)(2,1)S(1)}, bf16[448,128]{1,0:T(8,128)(2,1)S(1)}, u32[]{:S(2)}, u32[]{:S(2)}) collective-permute-start(bf16[448,128]{1,0:T(8,128)(2,1)S(1)} %fusion.3), channel_id=1, source_target_pairs={{0,4},{4,0},{8,12},{12,8},{16,20},{20,16},{24,28},{28,24},{1,5},{5... | collective-permute-start | bytes 344072 | tf_op jit(solution)/shard_map/ppermute | solution.py:211
  107.6 3.6 %collective-permute-start.21 = (bf16[896,128]{1,0:T(8,128)(2,1)S(1)}, bf16[896,128]{1,0:T(8,128)(2,1)S(1)}, u32[]{:S(2)}, u32[]{:S(2)}) collective-permute-start(bf16[896,128]{1,0:T(8,128)(2,1)S(1)} %fusion), channel_id=1, source_target_pairs={{0,2},{1,3},{2,0},{3,1},{4,6},{5,7},{6,4},{7,5},{8,10},{9,11},{10,... | collective-permute-start | bytes 688136 | tf_op jit(solution)/shard_map/ppermute | solution.py:211
  111.3 2.0 %collective-permute-start.33 = (bf16[224,128]{1,0:T(8,128)(2,1)S(1)}, bf16[224,128]{1,0:T(8,128)(2,1)S(1)}, u32[]{:S(2)}, u32[]{:S(2)}) collective-permute-start(bf16[224,128]{1,0:T(8,128)(2,1)S(1)} %fusion.5), channel_id=1, source_target_pairs={{0,8},{4,12},{8,0},{12,4},{16,24},{20,28},{24,16},{28,20},{1,9},{5... | collective-permute-start | bytes 172040 | tf_op jit(solution)/shard_map/ppermute | solution.py:211
  113.3 3.9 %collective-permute-done.21 = bf16[896,128]{1,0:T(8,128)(2,1)S(1)} collective-permute-done((bf16[896,128]{1,0:T(8,128)(2,1)S(1)}, bf16[896,128]{1,0:T(8,128)(2,1)S(1)}, u32[]{:S(2)}, u32[]{:S(2)}) %collective-permute-start.21) | collective-permute-done | bytes 229408 | tf_op jit(solution)/shard_map/ppermute | solution.py:211
  117.3 1.6 collective-permute-start.22
  119.0 1.3 collective-permute-start.34
  120.3 1.9 %collective-permute-done.22 = bf16[448,128]{1,0:T(8,128)(2,1)S(1)} collective-permute-done((bf16[448,128]{1,0:T(8,128)(2,1)S(1)}, bf16[448,128]{1,0:T(8,128)(2,1)S(1)}, u32[]{:S(2)}, u32[]{:S(2)}) %collective-permute-start.22) | collective-permute-done | bytes 114720 | tf_op jit(solution)/shard_map/ppermute | solution.py:211
  122.2 1.9 %collective-permute-start.23 = (bf16[224,128]{1,0:T(8,128)(2,1)S(1)}, bf16[224,128]{1,0:T(8,128)(2,1)S(1)}, u32[]{:S(2)}, u32[]{:S(2)}) collective-permute-start(bf16[224,128]{1,0:T(8,128)(2,1)S(1)} %fusion.4), channel_id=1, source_target_pairs={{0,8},{4,12},{8,0},{12,4},{16,24},{20,28},{24,16},{28,20},{1,9},{5... | collective-permute-start | bytes 172040 | tf_op jit(solution)/shard_map/ppermute | solution.py:211
  124.1 1.1 collective-permute-start.35
  125.1 1.6 collective-permute-done.23
  126.8 1.3 collective-permute-start.24
  128.1 1.1 collective-permute-done.35
  129.2 1.4 collective-permute-start.36
  130.6 1.2 collective-permute-done.24
  131.8 1.2 collective-permute-start.25
  133.5 1.9 %collective-permute-start.37 = (bf16[448,128]{1,0:T(8,128)(2,1)S(1)}, bf16[448,128]{1,0:T(8,128)(2,1)S(1)}, u32[]{:S(2)}, u32[]{:S(2)}) collective-permute-start(bf16[448,128]{1,0:T(8,128)(2,1)S(1)} %maximum_select_fusion.7), channel_id=1, source_target_pairs={{0,4},{4,0},{8,12},{12,8},{16,20},{20,16},{24,28},{28,24},{1,5},{5... | collective-permute-start | bytes 344072 | tf_op jit(solution)/shard_map/ppermute | solution.py:216
  135.4 1.3 collective-permute-start.17
  137.0 2.1 %collective-permute-start.26 = (bf16[224,128]{1,0:T(8,128)(2,1)S(1)}, bf16[224,128]{1,0:T(8,128)(2,1)S(1)}, u32[]{:S(2)}, u32[]{:S(2)}) collective-permute-start(bf16[224,128]{1,0:T(8,128)(2,1)S(1)} %maximum_select_fusion.8), channel_id=1, source_target_pairs={{0,8},{4,12},{8,0},{12,4},{16,24},{20,28},{24,16},{28,20},{1,9},{5... | collective-permute-start | bytes 172040 | tf_op jit(solution)/shard_map/ppermute | solution.py:216
  139.1 8.5 %collective-permute-done.37 = bf16[448,128]{1,0:T(8,128)(2,1)S(1)} collective-permute-done((bf16[448,128]{1,0:T(8,128)(2,1)S(1)}, bf16[448,128]{1,0:T(8,128)(2,1)S(1)}, u32[]{:S(2)}, u32[]{:S(2)}) %collective-permute-start.37) | collective-permute-done | bytes 114720 | tf_op jit(solution)/shard_map/ppermute | solution.py:216
  147.6 1.5 collective-permute-start.38
  149.1 2.5 %collective-permute-start.27 = (bf16[448,128]{1,0:T(8,128)(2,1)S(1)}, bf16[448,128]{1,0:T(8,128)(2,1)S(1)}, u32[]{:S(2)}, u32[]{:S(2)}) collective-permute-start(bf16[448,128]{1,0:T(8,128)(2,1)S(1)} %maximum_select_fusion.6), channel_id=1, source_target_pairs={{0,4},{4,0},{8,12},{12,8},{16,20},{20,16},{24,28},{28,24},{1,5},{5... | collective-permute-start | bytes 344072 | tf_op jit(solution)/shard_map/ppermute | solution.py:216
  151.7 1.3 collective-permute-start.15
  153.0 1.3 collective-permute-start.16
  154.5 3.5 %collective-permute-start.28 = (bf16[896,128]{1,0:T(8,128)(2,1)S(1)}, bf16[896,128]{1,0:T(8,128)(2,1)S(1)}, u32[]{:S(2)}, u32[]{:S(2)}) collective-permute-start(bf16[896,128]{1,0:T(8,128)(2,1)S(1)} %maximum_select_fusion.4), channel_id=1, source_target_pairs={{0,2},{1,3},{2,0},{3,1},{4,6},{5,7},{6,4},{7,5},{8,10},{9,11},{10,... | collective-permute-start | bytes 688136 | tf_op jit(solution)/shard_map/ppermute | solution.py:216
  158.3 0.7 collective-permute-start.18
  159.0 1.3 collective-permute-start.19
  160.3 6.8 %collective-permute-done.19.yb = bf16[2,1,256,128]{3,2,1,0:T(8,128)(2,1)S(1)} collective-permute-done((bf16[2,1,256,128]{3,2,1,0:T(8,128)(2,1)S(1)}, bf16[2,1,256,128]{3,2,1,0:T(8,128)(2,1)S(1)}, u32[]{:S(2)}, u32[]{:S(2)}) %collective-permute-start.19) | collective-permute-done | bytes 131104 | tf_op jit(solution)/shard_map/ppermute | solution.py:190
  167.1 0.6 copy-done.22
  168.0 5.6 %shard_map.79 = bf16[2,4,256,128]{3,2,1,0:T(8,128)(2,1)} custom-call(bf16[2,4,256,128]{3,2,1,0:T(8,128)(2,1)} %shard_map.78.x.d, bf16[2,1,256,128]{3,2,1,0:T(8,128)(2,1)} %copy-done.15, bf16[2,1,256,128]{3,2,1,0:T(8,128)(2,1)} %copy-done.16, bf16[2,4,256,128]{3,2,1,0:T(8,128)(2,1)} %copy-done.5, bf16[2,1,256,128]{3,2,1,0:T(8,128)(2,1)} %copy-done.21, ...), custom_call_target="tpu_custom_call" | custom-call | tf_op jit(solution)/shard_map/pallas_call | solution.py:50
  173.7 2.2 %collective-permute-start.29 = (bf16[1792,128]{1,0:T(8,128)(2,1)S(1)}, bf16[1792,128]{1,0:T(8,128)(2,1)S(1)}, u32[]{:S(2)}, u32[]{:S(2)}) collective-permute-start(bf16[1792,128]{1,0:T(8,128)(2,1)S(1)} %maximum_select_fusion.2), channel_id=1, source_target_pairs={{0,1},{1,0},{2,3},{3,2},{4,5},{5,4},{6,7},{7,6},{8,9},{9,8},{10,11... | collective-permute-start | bytes 1376264 | tf_op jit(solution)/shard_map/ppermute | solution.py:216
  176.2 1.4 convert.7
  177.9 1.4 convert.5
  (107 shorter events, 5.0 us)
Async XLA Ops:
  0.6 21.2 %collective-permute-start.2 = (bf16[2,4,256,128]{3,2,1,0:T(8,128)(2,1)}, bf16[2,4,256,128]{3,2,1,0:T(8,128)(2,1)S(1)}, u32[]{:S(2)}, u32[]{:S(2)}) collective-permute-start(bf16[2,4,256,128]{3,2,1,0:T(8,128)(2,1)} %x.3), channel_id=1, source_target_pairs={{0,4},{4,8},{8,12},{12,16},{16,20},{20,24},{24,28},{1,5},{5,9},{9,... | collective-permute-start | bytes 1572872 | tf_op jit(solution)/shard_map/ppermute | solution.py:186
  6.5 15.2 %collective-permute-start = (bf16[2,1,256,128]{3,2,1,0:T(8,128)(2,1)S(1)}, bf16[2,1,256,128]{3,2,1,0:T(8,128)(2,1)S(1)}, u32[]{:S(2)}, u32[]{:S(2)}) collective-permute-start(bf16[2,1,256,128]{3,2,1,0:T(8,128)(2,1)S(1)} %get-tuple-element.27), channel_id=1, source_target_pairs={{0,1},{1,2},{2,3},{4,5},{5,6},{6,7},{8,9},{9,10},{10,11},{12,13},{... | collective-permute-start | bytes 393224 | tf_op jit(solution)/shard_map/ppermute | solution.py:191
  8.0 13.8 %collective-permute-start.1 = (bf16[2,1,256,128]{3,2,1,0:T(8,128)(2,1)S(1)}, bf16[2,1,256,128]{3,2,1,0:T(8,128)(2,1)S(1)}, u32[]{:S(2)}, u32[]{:S(2)}) collective-permute-start(bf16[2,1,256,128]{3,2,1,0:T(8,128)(2,1)S(1)} %get-tuple-element.26), channel_id=1, source_target_pairs={{1,0},{2,1},{3,2},{5,4},{6,5},{7,6},{9,8},{10,9},{11,10},{13,12},{... | collective-permute-start | bytes 393224 | tf_op jit(solution)/shard_map/ppermute | solution.py:192
  9.3 12.5 %collective-permute-start.3 = (bf16[2,1,256,128]{3,2,1,0:T(8,128)(2,1)S(1)}, bf16[2,1,256,128]{3,2,1,0:T(8,128)(2,1)S(1)}, u32[]{:S(2)}, u32[]{:S(2)}) collective-permute-start(bf16[2,1,256,128]{3,2,1,0:T(8,128)(2,1)S(1)} %get-tuple-element.27), channel_id=1, source_target_pairs={{0,5},{1,6},{2,7},{4,9},{5,10},{6,11},{8,13},{9,14},{10,15},{12,17... | collective-permute-start | bytes 393224 | tf_op jit(solution)/shard_map/ppermute | solution.py:189
  15.1 6.8 %collective-permute-start.4 = (bf16[2,1,256,128]{3,2,1,0:T(8,128)(2,1)S(1)}, bf16[2,1,256,128]{3,2,1,0:T(8,128)(2,1)S(1)}, u32[]{:S(2)}, u32[]{:S(2)}) collective-permute-start(bf16[2,1,256,128]{3,2,1,0:T(8,128)(2,1)S(1)} %get-tuple-element.26), channel_id=1, source_target_pairs={{1,4},{2,5},{3,6},{5,8},{6,9},{7,10},{9,12},{10,13},{11,14},{13,16... | collective-permute-start | bytes 393224 | tf_op jit(solution)/shard_map/ppermute | solution.py:190
  21.8 0.7 copy-start.6
  21.8 0.7 copy-start.7
  21.8 0.7 copy-start.8
  21.8 0.7 copy-start.9
  21.9 0.9 copy-start.3
  28.9 19.8 %collective-permute-start.7 = (bf16[2,4,256,128]{3,2,1,0:T(8,128)(2,1)}, bf16[2,4,256,128]{3,2,1,0:T(8,128)(2,1)S(1)}, u32[]{:S(2)}, u32[]{:S(2)}) collective-permute-start(bf16[2,4,256,128]{3,2,1,0:T(8,128)(2,1)} %get-tuple-element.13.x), channel_id=1, source_target_pairs={{0,4},{4,8},{8,12},{12,16},{16,20},{20,24},{24,28},{1,5},{5,9},{9,... | collective-permute-start | bytes 1572872 | tf_op jit(solution)/shard_map/ppermute | solution.py:186
  34.0 12.4 %collective-permute-start.5 = (bf16[2,1,256,128]{3,2,1,0:T(8,128)(2,1)S(1)}, bf16[2,1,256,128]{3,2,1,0:T(8,128)(2,1)S(1)}, u32[]{:S(2)}, u32[]{:S(2)}) collective-permute-start(bf16[2,1,256,128]{3,2,1,0:T(8,128)(2,1)S(1)} %get-tuple-element.25), channel_id=1, source_target_pairs={{0,1},{1,2},{2,3},{4,5},{5,6},{6,7},{8,9},{9,10},{10,11},{12,13},{... | collective-permute-start | bytes 393224 | tf_op jit(solution)/shard_map/ppermute | solution.py:191
  37.9 8.5 %collective-permute-start.6 = (bf16[2,1,256,128]{3,2,1,0:T(8,128)(2,1)S(1)}, bf16[2,1,256,128]{3,2,1,0:T(8,128)(2,1)S(1)}, u32[]{:S(2)}, u32[]{:S(2)}) collective-permute-start(bf16[2,1,256,128]{3,2,1,0:T(8,128)(2,1)S(1)} %get-tuple-element.24), channel_id=1, source_target_pairs={{1,0},{2,1},{3,2},{5,4},{6,5},{7,6},{9,8},{10,9},{11,10},{13,12},{... | collective-permute-start | bytes 393224 | tf_op jit(solution)/shard_map/ppermute | solution.py:192
  39.2 9.5 %collective-permute-start.8 = (bf16[2,1,256,128]{3,2,1,0:T(8,128)(2,1)S(1)}, bf16[2,1,256,128]{3,2,1,0:T(8,128)(2,1)S(1)}, u32[]{:S(2)}, u32[]{:S(2)}) collective-permute-start(bf16[2,1,256,128]{3,2,1,0:T(8,128)(2,1)S(1)} %get-tuple-element.25), channel_id=1, source_target_pairs={{0,5},{1,6},{2,7},{4,9},{5,10},{6,11},{8,13},{9,14},{10,15},{12,17... | collective-permute-start | bytes 393224 | tf_op jit(solution)/shard_map/ppermute | solution.py:189
  45.7 3.0 %collective-permute-start.9 = (bf16[2,1,256,128]{3,2,1,0:T(8,128)(2,1)S(1)}, bf16[2,1,256,128]{3,2,1,0:T(8,128)(2,1)S(1)}, u32[]{:S(2)}, u32[]{:S(2)}) collective-permute-start(bf16[2,1,256,128]{3,2,1,0:T(8,128)(2,1)S(1)} %get-tuple-element.24), channel_id=1, source_target_pairs={{1,4},{2,5},{3,6},{5,8},{6,9},{7,10},{9,12},{10,13},{11,14},{13,16... | collective-permute-start | bytes 393224 | tf_op jit(solution)/shard_map/ppermute | solution.py:190
  46.4 2.3 %copy-start.10 = (bf16[2,1,256,128]{3,2,1,0:T(8,128)(2,1)}, bf16[2,1,256,128]{3,2,1,0:T(8,128)(2,1)S(1)}, u32[]{:S(2)}) copy-start(bf16[2,1,256,128]{3,2,1,0:T(8,128)(2,1)S(1)} %collective-permute-done.5.xt) | copy-start | bytes 393220
  46.4 2.3 %copy-start.11 = (bf16[2,1,256,128]{3,2,1,0:T(8,128)(2,1)}, bf16[2,1,256,128]{3,2,1,0:T(8,128)(2,1)S(1)}, u32[]{:S(2)}) copy-start(bf16[2,1,256,128]{3,2,1,0:T(8,128)(2,1)S(1)} %collective-permute-done.6.xb) | copy-start | bytes 393220
  48.7 0.7 copy-start.12
  48.7 0.7 copy-start.13
  48.7 0.9 copy-start.4
  55.9 9.2 %copy-start.2 = (bf16[2,4,256,128]{3,2,1,0:T(8,128)(2,1)S(1)}, bf16[2,4,256,128]{3,2,1,0:T(8,128)(2,1)}, u32[]{:S(2)}) copy-start(bf16[2,4,256,128]{3,2,1,0:T(8,128)(2,1)} %get-tuple-element.16.x.d) | copy-start | bytes 1572868
  62.5 7.8 %collective-permute-start.30 = (bf16[1792,128]{1,0:T(8,128)(2,1)S(1)}, bf16[1792,128]{1,0:T(8,128)(2,1)S(1)}, u32[]{:S(2)}, u32[]{:S(2)}) collective-permute-start(bf16[1792,128]{1,0:T(8,128)(2,1)S(1)} %dynamic-slice_bitcast_fusion), channel_id=1, source_target_pairs={{0,1},{1,0},{2,3},{3,2},{4,5},{5,4},{6,7},{7,6},{8,9},{9,8},{10,11... | collective-permute-start | bytes 1376264 | tf_op jit(solution)/shard_map/ppermute | solution.py:211
  65.1 7.9 %collective-permute-start.10 = (bf16[2,1,256,128]{3,2,1,0:T(8,128)(2,1)S(1)}, bf16[2,1,256,128]{3,2,1,0:T(8,128)(2,1)S(1)}, u32[]{:S(2)}, u32[]{:S(2)}) collective-permute-start(bf16[2,1,256,128]{3,2,1,0:T(8,128)(2,1)S(1)} %get-tuple-element.23), channel_id=1, source_target_pairs={{0,1},{1,2},{2,3},{4,5},{5,6},{6,7},{8,9},{9,10},{10,11},{12,13},{... | collective-permute-start | bytes 393224 | tf_op jit(solution)/shard_map/ppermute | solution.py:191
  67.0 12.1 %collective-permute-start.13 = (bf16[2,1,256,128]{3,2,1,0:T(8,128)(2,1)S(1)}, bf16[2,1,256,128]{3,2,1,0:T(8,128)(2,1)S(1)}, u32[]{:S(2)}, u32[]{:S(2)}) collective-permute-start(bf16[2,1,256,128]{3,2,1,0:T(8,128)(2,1)S(1)} %get-tuple-element.23), channel_id=1, source_target_pairs={{4,1},{5,2},{6,3},{8,5},{9,6},{10,7},{12,9},{13,10},{14,11},{16,13... | collective-permute-start | bytes 393224 | tf_op jit(solution)/shard_map/ppermute | solution.py:189
  67.7 11.4 %collective-permute-start.11 = (bf16[2,1,256,128]{3,2,1,0:T(8,128)(2,1)S(1)}, bf16[2,1,256,128]{3,2,1,0:T(8,128)(2,1)S(1)}, u32[]{:S(2)}, u32[]{:S(2)}) collective-permute-start(bf16[2,1,256,128]{3,2,1,0:T(8,128)(2,1)S(1)} %get-tuple-element.22), channel_id=1, source_target_pairs={{1,0},{2,1},{3,2},{5,4},{6,5},{7,6},{9,8},{10,9},{11,10},{13,12},{... | collective-permute-start | bytes 393224 | tf_op jit(solution)/shard_map/ppermute | solution.py:192
  69.0 11.9 %collective-permute-start.14 = (bf16[2,1,256,128]{3,2,1,0:T(8,128)(2,1)S(1)}, bf16[2,1,256,128]{3,2,1,0:T(8,128)(2,1)S(1)}, u32[]{:S(2)}, u32[]{:S(2)}) collective-permute-start(bf16[2,1,256,128]{3,2,1,0:T(8,128)(2,1)S(1)} %get-tuple-element.22), channel_id=1, source_target_pairs={{5,0},{6,1},{7,2},{9,4},{10,5},{11,6},{13,8},{14,9},{15,10},{17,12... | collective-permute-start | bytes 393224 | tf_op jit(solution)/shard_map/ppermute | solution.py:190
  70.3 20.7 %collective-permute-start.12 = (bf16[2,4,256,128]{3,2,1,0:T(8,128)(2,1)S(1)}, bf16[2,4,256,128]{3,2,1,0:T(8,128)(2,1)S(1)}, u32[]{:S(2)}, u32[]{:S(2)}) collective-permute-start(bf16[2,4,256,128]{3,2,1,0:T(8,128)(2,1)S(1)} %copy-done.2), channel_id=1, source_target_pairs={{4,0},{8,4},{12,8},{16,12},{20,16},{24,20},{28,24},{5,1},{9,5},{13... | collective-permute-start | bytes 1572872 | tf_op jit(solution)/shard_map/ppermute | solution.py:186
  73.0 18.1 %copy-start.17 = (bf16[2,1,256,128]{3,2,1,0:T(8,128)(2,1)}, bf16[2,1,256,128]{3,2,1,0:T(8,128)(2,1)S(1)}, u32[]{:S(2)}) copy-start(bf16[2,1,256,128]{3,2,1,0:T(8,128)(2,1)S(1)} %collective-permute-done.10.xt) | copy-start | bytes 393220
  73.0 31.8 %collective-permute-start.31 = (bf16[896,128]{1,0:T(8,128)(2,1)S(1)}, bf16[896,128]{1,0:T(8,128)(2,1)S(1)}, u32[]{:S(2)}, u32[]{:S(2)}) collective-permute-start(bf16[896,128]{1,0:T(8,128)(2,1)S(1)} %fusion.1), channel_id=1, source_target_pairs={{0,2},{1,3},{2,0},{3,1},{4,6},{5,7},{6,4},{7,5},{8,10},{9,11},{10,... | collective-permute-start | bytes 688136 | tf_op jit(solution)/shard_map/ppermute | solution.py:211
  79.1 12.0 %copy-start.19 = (bf16[2,1,256,128]{3,2,1,0:T(8,128)(2,1)}, bf16[2,1,256,128]{3,2,1,0:T(8,128)(2,1)S(1)}, u32[]{:S(2)}) copy-start(bf16[2,1,256,128]{3,2,1,0:T(8,128)(2,1)S(1)} %collective-permute-done.11.xb) | copy-start | bytes 393220
  79.1 11.9 %copy-start.18 = (bf16[2,1,256,128]{3,2,1,0:T(8,128)(2,1)}, bf16[2,1,256,128]{3,2,1,0:T(8,128)(2,1)S(1)}, u32[]{:S(2)}) copy-start(bf16[2,1,256,128]{3,2,1,0:T(8,128)(2,1)S(1)} %collective-permute-done.13.yt) | copy-start | bytes 393220
  80.9 10.2 %copy-start.20 = (bf16[2,1,256,128]{3,2,1,0:T(8,128)(2,1)}, bf16[2,1,256,128]{3,2,1,0:T(8,128)(2,1)S(1)}, u32[]{:S(2)}) copy-start(bf16[2,1,256,128]{3,2,1,0:T(8,128)(2,1)S(1)} %collective-permute-done.14.yb) | copy-start | bytes 393220
  91.0 0.8 copy-start.14
  103.2 4.2 %copy-start.1 = (bf16[4,896,128]{2,1,0:T(8,128)(2,1)S(1)}, bf16[4,896,128]{2,1,0:T(8,128)(2,1)}, u32[]{:S(2)}) copy-start(bf16[4,896,128]{2,1,0:T(8,128)(2,1)} %shard_map.80) | copy-start | bytes 2752516
  104.4 3.1 %collective-permute-start.20 = (bf16[1792,128]{1,0:T(8,128)(2,1)S(1)}, bf16[1792,128]{1,0:T(8,128)(2,1)S(1)}, u32[]{:S(2)}, u32[]{:S(2)}) collective-permute-start(bf16[1792,128]{1,0:T(8,128)(2,1)S(1)} %dynamic-slice_bitcast_fusion.1), channel_id=1, source_target_pairs={{0,1},{1,0},{2,3},{3,2},{4,5},{5,4},{6,7},{7,6},{8,9},{9,8},{10,11... | collective-permute-start | bytes 1376264 | tf_op jit(solution)/shard_map/ppermute | solution.py:211
  104.9 6.4 %collective-permute-start.32 = (bf16[448,128]{1,0:T(8,128)(2,1)S(1)}, bf16[448,128]{1,0:T(8,128)(2,1)S(1)}, u32[]{:S(2)}, u32[]{:S(2)}) collective-permute-start(bf16[448,128]{1,0:T(8,128)(2,1)S(1)} %fusion.3), channel_id=1, source_target_pairs={{0,4},{4,0},{8,12},{12,8},{16,20},{20,16},{24,28},{28,24},{1,5},{5... | collective-permute-start | bytes 344072 | tf_op jit(solution)/shard_map/ppermute | solution.py:211
  107.6 9.6 %collective-permute-start.21 = (bf16[896,128]{1,0:T(8,128)(2,1)S(1)}, bf16[896,128]{1,0:T(8,128)(2,1)S(1)}, u32[]{:S(2)}, u32[]{:S(2)}) collective-permute-start(bf16[896,128]{1,0:T(8,128)(2,1)S(1)} %fusion), channel_id=1, source_target_pairs={{0,2},{1,3},{2,0},{3,1},{4,6},{5,7},{6,4},{7,5},{8,10},{9,11},{10,... | collective-permute-start | bytes 688136 | tf_op jit(solution)/shard_map/ppermute | solution.py:211
  111.3 24.1 %copy-start = (bf16[2,4,256,128]{3,2,1,0:T(8,128)(2,1)S(1)}, bf16[2,4,256,128]{3,2,1,0:T(8,128)(2,1)}, u32[]{:S(2)}) copy-start(bf16[2,4,256,128]{3,2,1,0:T(8,128)(2,1)} %shard_map.78.x.d) | copy-start | bytes 1572868
  111.3 7.6 %collective-permute-start.33 = (bf16[224,128]{1,0:T(8,128)(2,1)S(1)}, bf16[224,128]{1,0:T(8,128)(2,1)S(1)}, u32[]{:S(2)}, u32[]{:S(2)}) collective-permute-start(bf16[224,128]{1,0:T(8,128)(2,1)S(1)} %fusion.5), channel_id=1, source_target_pairs={{0,8},{4,12},{8,0},{12,4},{16,24},{20,28},{24,16},{28,20},{1,9},{5... | collective-permute-start | bytes 172040 | tf_op jit(solution)/shard_map/ppermute | solution.py:211
  117.3 4.9 %collective-permute-start.22 = (bf16[448,128]{1,0:T(8,128)(2,1)S(1)}, bf16[448,128]{1,0:T(8,128)(2,1)S(1)}, u32[]{:S(2)}, u32[]{:S(2)}) collective-permute-start(bf16[448,128]{1,0:T(8,128)(2,1)S(1)} %fusion.2), channel_id=1, source_target_pairs={{0,4},{4,0},{8,12},{12,8},{16,20},{20,16},{24,28},{28,24},{1,5},{5... | collective-permute-start | bytes 344072 | tf_op jit(solution)/shard_map/ppermute | solution.py:211
  119.0 5.1 %collective-permute-start.34 = (bf16[112,128]{1,0:T(8,128)(2,1)S(1)}, bf16[112,128]{1,0:T(8,128)(2,1)S(1)}, u32[]{:S(2)}, u32[]{:S(2)}) collective-permute-start(bf16[112,128]{1,0:T(8,128)(2,1)S(1)} %fusion.9), channel_id=1, source_target_pairs={{0,16},{4,20},{8,24},{12,28},{16,0},{20,4},{24,8},{28,12},{1,17},{... | collective-permute-start | bytes 86024 | tf_op jit(solution)/shard_map/ppermute | solution.py:211
  122.2 4.5 %collective-permute-start.23 = (bf16[224,128]{1,0:T(8,128)(2,1)S(1)}, bf16[224,128]{1,0:T(8,128)(2,1)S(1)}, u32[]{:S(2)}, u32[]{:S(2)}) collective-permute-start(bf16[224,128]{1,0:T(8,128)(2,1)S(1)} %fusion.4), channel_id=1, source_target_pairs={{0,8},{4,12},{8,0},{12,4},{16,24},{20,28},{24,16},{28,20},{1,9},{5... | collective-permute-start | bytes 172040 | tf_op jit(solution)/shard_map/ppermute | solution.py:211
  124.1 5.1 %collective-permute-start.35 = (bf16[112,128]{1,0:T(8,128)(2,1)S(1)}, bf16[112,128]{1,0:T(8,128)(2,1)S(1)}, u32[]{:S(2)}, u32[]{:S(2)}) collective-permute-start(bf16[112,128]{1,0:T(8,128)(2,1)S(1)} %fusion.6), channel_id=1, source_target_pairs={{0,16},{4,20},{8,24},{12,28},{16,0},{20,4},{24,8},{28,12},{1,17},{... | collective-permute-start | bytes 86024 | tf_op jit(solution)/shard_map/ppermute | solution.py:216
  126.8 5.0 %collective-permute-start.24 = (bf16[112,128]{1,0:T(8,128)(2,1)S(1)}, bf16[112,128]{1,0:T(8,128)(2,1)S(1)}, u32[]{:S(2)}, u32[]{:S(2)}) collective-permute-start(bf16[112,128]{1,0:T(8,128)(2,1)S(1)} %fusion.8), channel_id=1, source_target_pairs={{0,16},{4,20},{8,24},{12,28},{16,0},{20,4},{24,8},{28,12},{1,17},{... | collective-permute-start | bytes 86024 | tf_op jit(solution)/shard_map/ppermute | solution.py:211
  129.2 4.2 %collective-permute-start.36 = (bf16[224,128]{1,0:T(8,128)(2,1)S(1)}, bf16[224,128]{1,0:T(8,128)(2,1)S(1)}, u32[]{:S(2)}, u32[]{:S(2)}) collective-permute-start(bf16[224,128]{1,0:T(8,128)(2,1)S(1)} %maximum_select_fusion.9), channel_id=1, source_target_pairs={{0,8},{4,12},{8,0},{12,4},{16,24},{20,28},{24,16},{28,20},{1,9},{5... | collective-permute-start | bytes 172040 | tf_op jit(solution)/shard_map/ppermute | solution.py:216
  131.8 5.1 %collective-permute-start.25 = (bf16[112,128]{1,0:T(8,128)(2,1)S(1)}, bf16[112,128]{1,0:T(8,128)(2,1)S(1)}, u32[]{:S(2)}, u32[]{:S(2)}) collective-permute-start(bf16[112,128]{1,0:T(8,128)(2,1)S(1)} %fusion.7), channel_id=1, source_target_pairs={{0,16},{4,20},{8,24},{12,28},{16,0},{20,4},{24,8},{28,12},{1,17},{... | collective-permute-start | bytes 86024 | tf_op jit(solution)/shard_map/ppermute | solution.py:216
  133.5 14.0 %collective-permute-start.37 = (bf16[448,128]{1,0:T(8,128)(2,1)S(1)}, bf16[448,128]{1,0:T(8,128)(2,1)S(1)}, u32[]{:S(2)}, u32[]{:S(2)}) collective-permute-start(bf16[448,128]{1,0:T(8,128)(2,1)S(1)} %maximum_select_fusion.7), channel_id=1, source_target_pairs={{0,4},{4,0},{8,12},{12,8},{16,20},{20,16},{24,28},{28,24},{1,5},{5... | collective-permute-start | bytes 344072 | tf_op jit(solution)/shard_map/ppermute | solution.py:216
  135.4 31.7 %collective-permute-start.17 = (bf16[2,4,256,128]{3,2,1,0:T(8,128)(2,1)S(1)}, bf16[2,4,256,128]{3,2,1,0:T(8,128)(2,1)S(1)}, u32[]{:S(2)}, u32[]{:S(2)}) collective-permute-start(bf16[2,4,256,128]{3,2,1,0:T(8,128)(2,1)S(1)} %copy-done), channel_id=1, source_target_pairs={{4,0},{8,4},{12,8},{16,12},{20,16},{24,20},{28,24},{5,1},{9,5},{13... | collective-permute-start | bytes 1572872 | tf_op jit(solution)/shard_map/ppermute | solution.py:186
  137.0 12.1 %collective-permute-start.26 = (bf16[224,128]{1,0:T(8,128)(2,1)S(1)}, bf16[224,128]{1,0:T(8,128)(2,1)S(1)}, u32[]{:S(2)}, u32[]{:S(2)}) collective-permute-start(bf16[224,128]{1,0:T(8,128)(2,1)S(1)} %maximum_select_fusion.8), channel_id=1, source_target_pairs={{0,8},{4,12},{8,0},{12,4},{16,24},{20,28},{24,16},{28,20},{1,9},{5... | collective-permute-start | bytes 172040 | tf_op jit(solution)/shard_map/ppermute | solution.py:216
  147.6 10.4 %collective-permute-start.38 = (bf16[896,128]{1,0:T(8,128)(2,1)S(1)}, bf16[896,128]{1,0:T(8,128)(2,1)S(1)}, u32[]{:S(2)}, u32[]{:S(2)}) collective-permute-start(bf16[896,128]{1,0:T(8,128)(2,1)S(1)} %maximum_select_fusion.5), channel_id=1, source_target_pairs={{0,2},{1,3},{2,0},{3,1},{4,6},{5,7},{6,4},{7,5},{8,10},{9,11},{10,... | collective-permute-start | bytes 688136 | tf_op jit(solution)/shard_map/ppermute | solution.py:216
  149.1 5.3 %collective-permute-start.27 = (bf16[448,128]{1,0:T(8,128)(2,1)S(1)}, bf16[448,128]{1,0:T(8,128)(2,1)S(1)}, u32[]{:S(2)}, u32[]{:S(2)}) collective-permute-start(bf16[448,128]{1,0:T(8,128)(2,1)S(1)} %maximum_select_fusion.6), channel_id=1, source_target_pairs={{0,4},{4,0},{8,12},{12,8},{16,20},{20,16},{24,28},{28,24},{1,5},{5... | collective-permute-start | bytes 344072 | tf_op jit(solution)/shard_map/ppermute | solution.py:216
  151.7 6.6 %collective-permute-start.15 = (bf16[2,1,256,128]{3,2,1,0:T(8,128)(2,1)S(1)}, bf16[2,1,256,128]{3,2,1,0:T(8,128)(2,1)S(1)}, u32[]{:S(2)}, u32[]{:S(2)}) collective-permute-start(bf16[2,1,256,128]{3,2,1,0:T(8,128)(2,1)S(1)} %get-tuple-element.21), channel_id=1, source_target_pairs={{0,1},{1,2},{2,3},{4,5},{5,6},{6,7},{8,9},{9,10},{10,11},{12,13},{... | collective-permute-start | bytes 393224 | tf_op jit(solution)/shard_map/ppermute | solution.py:191
  153.0 6.0 %collective-permute-start.16 = (bf16[2,1,256,128]{3,2,1,0:T(8,128)(2,1)S(1)}, bf16[2,1,256,128]{3,2,1,0:T(8,128)(2,1)S(1)}, u32[]{:S(2)}, u32[]{:S(2)}) collective-permute-start(bf16[2,1,256,128]{3,2,1,0:T(8,128)(2,1)S(1)} %get-tuple-element.20), channel_id=1, source_target_pairs={{1,0},{2,1},{3,2},{5,4},{6,5},{7,6},{9,8},{10,9},{11,10},{13,12},{... | collective-permute-start | bytes 393224 | tf_op jit(solution)/shard_map/ppermute | solution.py:192
  154.5 19.1 %collective-permute-start.28 = (bf16[896,128]{1,0:T(8,128)(2,1)S(1)}, bf16[896,128]{1,0:T(8,128)(2,1)S(1)}, u32[]{:S(2)}, u32[]{:S(2)}) collective-permute-start(bf16[896,128]{1,0:T(8,128)(2,1)S(1)} %maximum_select_fusion.4), channel_id=1, source_target_pairs={{0,2},{1,3},{2,0},{3,1},{4,6},{5,7},{6,4},{7,5},{8,10},{9,11},{10,... | collective-permute-start | bytes 688136 | tf_op jit(solution)/shard_map/ppermute | solution.py:216
  158.2 17.7 %collective-permute-start.39 = (bf16[1792,128]{1,0:T(8,128)(2,1)S(1)}, bf16[1792,128]{1,0:T(8,128)(2,1)S(1)}, u32[]{:S(2)}, u32[]{:S(2)}) collective-permute-start(bf16[1792,128]{1,0:T(8,128)(2,1)S(1)} %maximum_select_fusion.3), channel_id=1, source_target_pairs={{0,1},{1,0},{2,3},{3,2},{4,5},{5,4},{6,7},{7,6},{8,9},{9,8},{10,11... | collective-permute-start | bytes 1376264 | tf_op jit(solution)/shard_map/ppermute | solution.py:216
  158.3 8.9 %copy-start.15 = (bf16[2,1,256,128]{3,2,1,0:T(8,128)(2,1)}, bf16[2,1,256,128]{3,2,1,0:T(8,128)(2,1)S(1)}, u32[]{:S(2)}) copy-start(bf16[2,1,256,128]{3,2,1,0:T(8,128)(2,1)S(1)} %collective-permute-done.15.xt) | copy-start | bytes 393220
  158.3 2.0 %collective-permute-start.18 = (bf16[2,1,256,128]{3,2,1,0:T(8,128)(2,1)S(1)}, bf16[2,1,256,128]{3,2,1,0:T(8,128)(2,1)S(1)}, u32[]{:S(2)}, u32[]{:S(2)}) collective-permute-start(bf16[2,1,256,128]{3,2,1,0:T(8,128)(2,1)S(1)} %get-tuple-element.21), channel_id=1, source_target_pairs={{4,1},{5,2},{6,3},{8,5},{9,6},{10,7},{12,9},{13,10},{14,11},{16,13... | collective-permute-start | bytes 393224 | tf_op jit(solution)/shard_map/ppermute | solution.py:189
  159.0 8.2 %copy-start.16 = (bf16[2,1,256,128]{3,2,1,0:T(8,128)(2,1)}, bf16[2,1,256,128]{3,2,1,0:T(8,128)(2,1)S(1)}, u32[]{:S(2)}) copy-start(bf16[2,1,256,128]{3,2,1,0:T(8,128)(2,1)S(1)} %collective-permute-done.16.xb) | copy-start | bytes 393220
  159.0 8.2 %collective-permute-start.19 = (bf16[2,1,256,128]{3,2,1,0:T(8,128)(2,1)S(1)}, bf16[2,1,256,128]{3,2,1,0:T(8,128)(2,1)S(1)}, u32[]{:S(2)}, u32[]{:S(2)}) collective-permute-start(bf16[2,1,256,128]{3,2,1,0:T(8,128)(2,1)S(1)} %get-tuple-element.20), channel_id=1, source_target_pairs={{5,0},{6,1},{7,2},{9,4},{10,5},{11,6},{13,8},{14,9},{15,10},{17,12... | collective-permute-start | bytes 393224 | tf_op jit(solution)/shard_map/ppermute | solution.py:190
  160.3 6.9 %copy-start.21 = (bf16[2,1,256,128]{3,2,1,0:T(8,128)(2,1)}, bf16[2,1,256,128]{3,2,1,0:T(8,128)(2,1)S(1)}, u32[]{:S(2)}) copy-start(bf16[2,1,256,128]{3,2,1,0:T(8,128)(2,1)S(1)} %collective-permute-done.18.yt) | copy-start | bytes 393220
  167.1 0.7 copy-start.22
  167.1 0.8 copy-start.5
  173.7 3.9 %collective-permute-start.29 = (bf16[1792,128]{1,0:T(8,128)(2,1)S(1)}, bf16[1792,128]{1,0:T(8,128)(2,1)S(1)}, u32[]{:S(2)}, u32[]{:S(2)}) collective-permute-start(bf16[1792,128]{1,0:T(8,128)(2,1)S(1)} %maximum_select_fusion.2), channel_id=1, source_target_pairs={{0,1},{1,0},{2,3},{3,2},{4,5},{5,4},{6,7},{7,6},{8,9},{9,8},{10,11... | collective-permute-start | bytes 1376264 | tf_op jit(solution)/shard_map/ppermute | solution.py:216
where the time goes:
time: 180 us; the launch traced here: 179 us
  starting transfers between devices  83.9 us (47%)
  Pallas kernels  41 us (23%)
  waiting for transfers between devices  40 us (22%)
  local copies, waits for them, and re-layouts  7.93 us (4%)
  other arithmetic  5.17 us (3%)
    pallas_call x7, Pallas kernels, call(): pl.pallas_call(body, out_shape=outs, scratch_shapes=scratch, compiler_par...  41 us
    ppermute x10, starting transfers between devices, reduced(): part = kept + lax.ppermute(sent, axis, pairs).astype(F32)  23.5 us
    ppermute x10, starting transfers between devices, reduced(): got = lax.ppermute(part, axis, pairs)  17.4 us
    ppermute x4, starting transfers between devices, exchanged(): other_top = lax.ppermute(near_bottom, both, down)  13.6 us
    ppermute x4, starting transfers between devices, exchanged(): other = lax.ppermute(near, 'frame', along)  11.7 us
    ppermute x10, waiting for transfers between devices, reduced(): got = lax.ppermute(part, axis, pairs)  10.5 us
    ppermute x4, waiting for transfers between devices, exchanged(): other = lax.ppermute(near, 'frame', along)  10.2 us
    ppermute x4, starting transfers between devices, exchanged(): own_top = lax.ppermute(bottom, 'row', [(j, j + 1) for j in range(rows - 1)])  8.62 us
  transfers between devices with their start and end apart: 40, of which 13 were waited for; matrix products, arithmetic and copies ran while one was open for 4% of the time, Pallas kernels for 13%

commit v1 on v0

--- a/solution.py
+++ b/solution.py
@@ -51,7 +51,7 @@
         body,
         out_shape=outs,
         scratch_shapes=scratch,
-        compiler_params=pltpu.CompilerParams(vmem_limit_bytes=56 << 20),
+        compiler_params=pltpu.CompilerParams(vmem_limit_bytes=28 << 20),
     )(*args)
 
 
@@ -235,10 +235,12 @@
     act_near = exchanged(act, 1)
     critic_map, second_delta = second_layer(*act_near, second_ahead, cotangent)
     second_near = exchanged(second_delta, -1)
-    second_grad = finish(weight_grad(*act_near, second_delta, grad_scale, n_row, padded))
+    second_part = weight_grad(*act_near, second_delta, grad_scale, n_row, padded)
+    second_grad = finish(second_part)
     first_delta = input_grad(*second_near, second_back, slope)
     first_near = exchanged(first_delta, -1)
-    first_grad = finish(weight_grad(*clip_near, first_delta, grad_scale, n_row, padded))
+    first_part = weight_grad(*clip_near, first_delta, grad_scale, n_row, padded)
+    first_grad = finish(first_part)
     clip_grad = input_grad(*first_near, first_back)
     return critic_map, clip_grad, first_grad, second_grad
 

time: 180 us -> 175 us (0.972)
  Pallas kernels: 41 us -> 21.4 us
  local copies, waits for them, and re-layouts: 7.93 us -> 17.8 us
  other arithmetic: 5.17 us -> 12.1 us
  starting transfers between devices: 83.9 us -> 80.8 us
    pallas_call x7, Pallas kernels: 41 us -> 21.4 us  [call(): pl.pallas_call(body, out_shape=outs, scratch_shapes=scratch, compiler_par...]
    unnamed x46 -> x64, local copies, waits for them, and re-layouts: 3.44 us -> 14.9 us
    select_n x10, other arithmetic: 0.97 us -> 6.97 us  [reduced(): jnp.where(mine == 0, jnp.concatenate([part, got]), jnp.concatenate([got,...]
    ppermute x10, starting transfers between devices: 17.4 us -> 14.1 us  [reduced(): got = lax.ppermute(part, axis, pairs)]
    squeeze x2, local copies, waits for them, and re-layouts: 2.18 us -> 0.08 us  [reduced(): sent = lax.dynamic_index_in_dim(halves, 1 - mine, 0, False).astype(BF)]
    ppermute x10, waiting for transfers between devices: 8.52 us -> 10.4 us  [reduced(): part = kept + lax.ppermute(sent, axis, pairs).astype(F32)]
    ppermute x4, waiting for transfers between devices: 8.59 us -> 6.76 us  [exchanged(): other_bottom = lax.ppermute(near_top, both, up)]
  transfers between devices with their start and end apart: 40 -> 40, of which waited for: 13 -> 12; matrix products, arithmetic and copies ran while one was open for 4% -> 8% of each run, Pallas kernels for 13% -> 7%
where the time goes in v1:
time: 175 us; the launch traced here: 174 us
  starting transfers between devices  80.8 us (46%)
  waiting for transfers between devices  40.5 us (23%)
  Pallas kernels  21.4 us (12%)
  local copies, waits for them, and re-layouts  17.8 us (10%)
  other arithmetic  12.1 us (7%)
    ppermute x10, starting transfers between devices, reduced(): part = kept + lax.ppermute(sent, axis, pairs).astype(F32)  22.8 us
    pallas_call x7, Pallas kernels, call(): pl.pallas_call(body, out_shape=outs, scratch_shapes=scratch, compiler_par...  21.4 us
    unnamed x64, local copies, waits for them, and re-layouts  14.9 us
    ppermute x4, starting transfers between devices, exchanged(): other_top = lax.ppermute(near_bottom, both, down)  14.2 us
    ppermute x10, starting transfers between devices, reduced(): got = lax.ppermute(part, axis, pairs)  14.1 us
    ppermute x4, starting transfers between devices, exchanged(): other = lax.ppermute(near, 'frame', along)  11.8 us
    ppermute x10, waiting for transfers between devices, reduced(): got = lax.ppermute(part, axis, pairs)  10.8 us
    ppermute x10, waiting for transfers between devices, reduced(): part = kept + lax.ppermute(sent, axis, pairs).astype(F32)  10.4 us
  transfers between devices with their start and end apart: 40, of which 12 were waited for; matrix products, arithmetic and copies ran while one was open for 8% of the time, Pallas kernels for 7%

profile of v1, /device:TPU:0, one launch (start us, length us, event | category | flops | bytes accessed | tf_op | source)
XLA Modules:
  0.0 173.9 jit_solution(1195605886892300278)
XLA Ops:
  0.6 5.0 %collective-permute-start.2 = (bf16[2,4,256,128]{3,2,1,0:T(8,128)(2,1)}, bf16[2,4,256,128]{3,2,1,0:T(8,128)(2,1)S(1)}, u32[]{:S(2)}, u32[]{:S(2)}) collective-permute-start(bf16[2,4,256,128]{3,2,1,0:T(8,128)(2,1)} %x.3), channel_id=1, source_target_pairs={{0,4},{4,8},{8,12},{12,16},{16,20},{20,24},{24,28},{1,5},{5,9},{9,... | collective-permute-start | bytes 1572872 | tf_op jit(solution)/shard_map/ppermute | solution.py:186
  5.7 1.0 fusion.13
  6.7 1.5 collective-permute-start
  8.2 1.3 collective-permute-start.1
  9.5 5.7 %collective-permute-start.3 = (bf16[2,1,256,128]{3,2,1,0:T(8,128)(2,1)S(1)}, bf16[2,1,256,128]{3,2,1,0:T(8,128)(2,1)S(1)}, u32[]{:S(2)}, u32[]{:S(2)}) collective-permute-start(bf16[2,1,256,128]{3,2,1,0:T(8,128)(2,1)S(1)} %get-tuple-element.27), channel_id=1, source_target_pairs={{0,5},{1,6},{2,7},{4,9},{5,10},{6,11},{8,13},{9,14},{10,15},{12,17... | collective-permute-start | bytes 393224 | tf_op jit(solution)/shard_map/ppermute | solution.py:189
  15.9 1.2 copy-done.9
  17.1 1.2 copy-done.10
  18.2 1.6 shard_map.75
  19.8 1.4 copy-done.1
  21.2 1.4 copy-done.5
  22.7 2.9 %shard_map.76 = (bf16[2,4,256,128]{3,2,1,0:T(8,128)(2,1)S(1)}, f32[2,4,256,128]{3,2,1,0:T(8,128)S(1)}) custom-call(bf16[2,4,256,128]{3,2,1,0:T(8,128)(2,1)S(1)} %copy-done, bf16[2,1,256,128]{3,2,1,0:T(8,128)(2,1)S(1)} %collective-permute-done.xt, bf16[2,1,256,128]{3,2,1,0:T(8,128)(2,1)S(1)} %collective-permute-done.1.xb, ...), custom_call_target="tpu_custom_call" | custom-call | tf_op jit(solution)/shard_map/pallas_call | solution.py:50
  25.7 1.0 copy-done.7
  26.6 4.0 %collective-permute-start.7 = (bf16[2,4,256,128]{3,2,1,0:T(8,128)(2,1)S(1)}, bf16[2,4,256,128]{3,2,1,0:T(8,128)(2,1)S(1)}, u32[]{:S(2)}, u32[]{:S(2)}) collective-permute-start(bf16[2,4,256,128]{3,2,1,0:T(8,128)(2,1)S(1)} %get-tuple-element.13.x), channel_id=1, source_target_pairs={{0,4},{4,8},{8,12},{12,16},{16,20},{20,24},{24,28},{1,5},{5,9},{9,... | collective-permute-start | bytes 1572872 | tf_op jit(solution)/shard_map/ppermute | solution.py:186
  30.7 3.9 %collective-permute-start.5 = (bf16[2,1,256,128]{3,2,1,0:T(8,128)(2,1)S(1)}, bf16[2,1,256,128]{3,2,1,0:T(8,128)(2,1)S(1)}, u32[]{:S(2)}, u32[]{:S(2)}) collective-permute-start(bf16[2,1,256,128]{3,2,1,0:T(8,128)(2,1)S(1)} %get-tuple-element.25), channel_id=1, source_target_pairs={{0,1},{1,2},{2,3},{4,5},{5,6},{6,7},{8,9},{9,10},{10,11},{12,13},{... | collective-permute-start | bytes 393224 | tf_op jit(solution)/shard_map/ppermute | solution.py:191
  34.6 1.3 collective-permute-start.6
  35.9 6.5 %collective-permute-start.8 = (bf16[2,1,256,128]{3,2,1,0:T(8,128)(2,1)S(1)}, bf16[2,1,256,128]{3,2,1,0:T(8,128)(2,1)S(1)}, u32[]{:S(2)}, u32[]{:S(2)}) collective-permute-start(bf16[2,1,256,128]{3,2,1,0:T(8,128)(2,1)S(1)} %get-tuple-element.25), channel_id=1, source_target_pairs={{0,5},{1,6},{2,7},{4,9},{5,10},{6,11},{8,13},{9,14},{10,15},{12,17... | collective-permute-start | bytes 393224 | tf_op jit(solution)/shard_map/ppermute | solution.py:189
  43.2 2.3 %collective-permute-done.8.yt = bf16[2,1,256,128]{3,2,1,0:T(8,128)(2,1)S(1)} collective-permute-done((bf16[2,1,256,128]{3,2,1,0:T(8,128)(2,1)S(1)}, bf16[2,1,256,128]{3,2,1,0:T(8,128)(2,1)S(1)}, u32[]{:S(2)}, u32[]{:S(2)}) %collective-permute-start.8) | collective-permute-done | bytes 131104 | tf_op jit(solution)/shard_map/ppermute | solution.py:189
  46.1 1.7 copy-done.4
  48.7 3.7 %shard_map.77 = (bf16[2,4,256,128]{3,2,1,0:T(8,128)(2,1)}, bf16[2,4,256,128]{3,2,1,0:T(8,128)(2,1)S(1)}) custom-call(bf16[2,4,256,128]{3,2,1,0:T(8,128)(2,1)S(1)} %get-tuple-element.13.x, bf16[2,1,256,128]{3,2,1,0:T(8,128)(2,1)S(1)} %collective-permute-done.5.xt, bf16[2,1,256,128]{3,2,1,0:T(8,128)(2,1)S(1)} %collective-permute-done.6.xb, ...), custom_call_target="tpu_custom_call" | custom-call | tf_op jit(solution)/shard_map/pallas_call | solution.py:50
  55.2 3.1 %shard_map.81 = bf16[4,896,128]{2,1,0:T(8,128)(2,1)S(1)} custom-call(bf16[2,4,256,128]{3,2,1,0:T(8,128)(2,1)S(1)} %get-tuple-element.13.x, bf16[2,1,256,128]{3,2,1,0:T(8,128)(2,1)S(1)} %copy-done.21, bf16[2,1,256,128]{3,2,1,0:T(8,128)(2,1)S(1)} %copy-done.23, bf16[2,4,256,128]{3,2,1,0:T(8,128)(2,1)S(1)} %collective-permute-done.7.y, ...), custom_call_target="tpu_custom_call" | custom-call | tf_op jit(solution)/shard_map/pallas_call | solution.py:50
  58.3 2.5 %collective-permute-start.30 = (bf16[1792,128]{1,0:T(8,128)(2,1)S(1)}, bf16[1792,128]{1,0:T(8,128)(2,1)}, u32[]{:S(2)}, u32[]{:S(2)}) collective-permute-start(bf16[1792,128]{1,0:T(8,128)(2,1)S(1)} %dynamic-slice_bitcast_fusion), channel_id=1, source_target_pairs={{0,1},{1,0},{2,3},{3,2},{4,5},{5,4},{6,7},{7,6},{8,9},{9,8},{10,11... | collective-permute-start | bytes 1376264 | tf_op jit(solution)/shard_map/ppermute | solution.py:211
  60.8 2.1 %collective-permute-start.10 = (bf16[2,1,256,128]{3,2,1,0:T(8,128)(2,1)S(1)}, bf16[2,1,256,128]{3,2,1,0:T(8,128)(2,1)S(1)}, u32[]{:S(2)}, u32[]{:S(2)}) collective-permute-start(bf16[2,1,256,128]{3,2,1,0:T(8,128)(2,1)S(1)} %get-tuple-element.23), channel_id=1, source_target_pairs={{0,1},{1,2},{2,3},{4,5},{5,6},{6,7},{8,9},{9,10},{10,11},{12,13},{... | collective-permute-start | bytes 393224 | tf_op jit(solution)/shard_map/ppermute | solution.py:191
  63.6 1.3 collective-permute-start.11
  64.9 1.3 collective-permute-start.14
  66.2 1.5 collective-permute-start.12
  67.7 1.1 convert_add_fusion
  69.6 6.1 %collective-permute-start.31 = (bf16[896,128]{1,0:T(8,128)(2,1)}, bf16[896,128]{1,0:T(8,128)(2,1)}, u32[]{:S(2)}, u32[]{:S(2)}) collective-permute-start(bf16[896,128]{1,0:T(8,128)(2,1)} %fusion.1), channel_id=1, source_target_pairs={{0,2},{1,3},{2,0},{3,1},{4,6},{5,7},{6,4},{7,5},{8,10},{9,11},{10,... | collective-permute-start | bytes 688136 | tf_op jit(solution)/shard_map/ppermute | solution.py:211
  75.7 1.1 collective-permute-done.14.yb
  76.8 10.2 %collective-permute-done.12.y = bf16[2,4,256,128]{3,2,1,0:T(8,128)(2,1)S(1)} collective-permute-done((bf16[2,4,256,128]{3,2,1,0:T(8,128)(2,1)S(1)}, bf16[2,4,256,128]{3,2,1,0:T(8,128)(2,1)S(1)}, u32[]{:S(2)}, u32[]{:S(2)}) %collective-permute-start.12) | collective-permute-done | bytes 524320 | tf_op jit(solution)/shard_map/ppermute | solution.py:186
  87.0 1.2 copy-done.8
  88.2 2.6 %shard_map.78.x.d = bf16[2,4,256,128]{3,2,1,0:T(8,128)(2,1)S(1)} custom-call(bf16[2,4,256,128]{3,2,1,0:T(8,128)(2,1)S(1)} %get-tuple-element.16.x.d, bf16[2,1,256,128]{3,2,1,0:T(8,128)(2,1)S(1)} %collective-permute-done.10.xt, bf16[2,1,256,128]{3,2,1,0:T(8,128)(2,1)S(1)} %collective-permute-done.11.xb, ...), custom_call_target="tpu_custom_call" | custom-call | tf_op jit(solution)/shard_map/pallas_call | solution.py:50
  90.9 3.1 %shard_map.80 = bf16[4,896,128]{2,1,0:T(8,128)(2,1)S(1)} custom-call(bf16[2,4,256,128]{3,2,1,0:T(8,128)(2,1)S(1)} %copy-done, bf16[2,1,256,128]{3,2,1,0:T(8,128)(2,1)S(1)} %copy-done.13, bf16[2,1,256,128]{3,2,1,0:T(8,128)(2,1)S(1)} %copy-done.15, bf16[2,4,256,128]{3,2,1,0:T(8,128)(2,1)S(1)} %collective-permute-done.2.y, ...), custom_call_target="tpu_custom_call" | custom-call | tf_op jit(solution)/shard_map/pallas_call | solution.py:50
  94.4 1.0 bitcast_add_fusion
  95.5 2.6 %collective-permute-start.32 = (bf16[448,128]{1,0:T(8,128)(2,1)S(1)}, bf16[448,128]{1,0:T(8,128)(2,1)S(1)}, u32[]{:S(2)}, u32[]{:S(2)}) collective-permute-start(bf16[448,128]{1,0:T(8,128)(2,1)S(1)} %fusion.3), channel_id=1, source_target_pairs={{0,4},{4,0},{8,12},{12,8},{16,20},{20,16},{24,28},{28,24},{1,5},{5... | collective-permute-start | bytes 344072 | tf_op jit(solution)/shard_map/ppermute | solution.py:211
  98.2 3.7 %collective-permute-start.21 = (bf16[896,128]{1,0:T(8,128)(2,1)S(1)}, bf16[896,128]{1,0:T(8,128)(2,1)S(1)}, u32[]{:S(2)}, u32[]{:S(2)}) collective-permute-start(bf16[896,128]{1,0:T(8,128)(2,1)S(1)} %fusion), channel_id=1, source_target_pairs={{0,2},{1,3},{2,0},{3,1},{4,6},{5,7},{6,4},{7,5},{8,10},{9,11},{10,... | collective-permute-start | bytes 688136 | tf_op jit(solution)/shard_map/ppermute | solution.py:211
  101.9 2.0 %collective-permute-start.33 = (bf16[224,128]{1,0:T(8,128)(2,1)S(1)}, bf16[224,128]{1,0:T(8,128)(2,1)S(1)}, u32[]{:S(2)}, u32[]{:S(2)}) collective-permute-start(bf16[224,128]{1,0:T(8,128)(2,1)S(1)} %fusion.5), channel_id=1, source_target_pairs={{0,8},{4,12},{8,0},{12,4},{16,24},{20,28},{24,16},{28,20},{1,9},{5... | collective-permute-start | bytes 172040 | tf_op jit(solution)/shard_map/ppermute | solution.py:211
  103.9 3.9 %collective-permute-done.21 = bf16[896,128]{1,0:T(8,128)(2,1)S(1)} collective-permute-done((bf16[896,128]{1,0:T(8,128)(2,1)S(1)}, bf16[896,128]{1,0:T(8,128)(2,1)S(1)}, u32[]{:S(2)}, u32[]{:S(2)}) %collective-permute-start.21) | collective-permute-done | bytes 229408 | tf_op jit(solution)/shard_map/ppermute | solution.py:211
  108.6 1.6 collective-permute-start.34
  110.2 2.5 %collective-permute-done.22 = bf16[448,128]{1,0:T(8,128)(2,1)S(1)} collective-permute-done((bf16[448,128]{1,0:T(8,128)(2,1)S(1)}, bf16[448,128]{1,0:T(8,128)(2,1)S(1)}, u32[]{:S(2)}, u32[]{:S(2)}) %collective-permute-start.22) | collective-permute-done | bytes 114720 | tf_op jit(solution)/shard_map/ppermute | solution.py:211
  112.8 1.8 %collective-permute-start.23 = (bf16[224,128]{1,0:T(8,128)(2,1)S(1)}, bf16[224,128]{1,0:T(8,128)(2,1)S(1)}, u32[]{:S(2)}, u32[]{:S(2)}) collective-permute-start(bf16[224,128]{1,0:T(8,128)(2,1)S(1)} %fusion.4), channel_id=1, source_target_pairs={{0,8},{4,12},{8,0},{12,4},{16,24},{20,28},{24,16},{28,20},{1,9},{5... | collective-permute-start | bytes 172040 | tf_op jit(solution)/shard_map/ppermute | solution.py:211
  115.1 2.2 %collective-permute-done.23 = bf16[224,128]{1,0:T(8,128)(2,1)S(1)} collective-permute-done((bf16[224,128]{1,0:T(8,128)(2,1)S(1)}, bf16[224,128]{1,0:T(8,128)(2,1)S(1)}, u32[]{:S(2)}, u32[]{:S(2)}) %collective-permute-start.23) | collective-permute-done | bytes 57376 | tf_op jit(solution)/shard_map/ppermute | solution.py:211
  117.4 1.3 collective-permute-start.24
  118.7 1.5 collective-permute-done.35
  120.5 1.8 %collective-permute-done.24 = bf16[112,128]{1,0:T(8,128)(2,1)S(1)} collective-permute-done((bf16[112,128]{1,0:T(8,128)(2,1)S(1)}, bf16[112,128]{1,0:T(8,128)(2,1)S(1)}, u32[]{:S(2)}, u32[]{:S(2)}) %collective-permute-start.24) | collective-permute-done | bytes 28704 | tf_op jit(solution)/shard_map/ppermute | solution.py:211
  122.3 1.3 collective-permute-start.25
  124.6 1.3 collective-permute-start.17
  125.9 1.7 collective-permute-done.25
  128.4 2.5 %collective-permute-start.26 = (bf16[224,128]{1,0:T(8,128)(2,1)S(1)}, bf16[224,128]{1,0:T(8,128)(2,1)S(1)}, u32[]{:S(2)}, u32[]{:S(2)}) collective-permute-start(bf16[224,128]{1,0:T(8,128)(2,1)S(1)} %maximum_select_fusion.8), channel_id=1, source_target_pairs={{0,8},{4,12},{8,0},{12,4},{16,24},{20,28},{24,16},{28,20},{1,9},{5... | collective-permute-start | bytes 172040 | tf_op jit(solution)/shard_map/ppermute | solution.py:216
  130.8 6.8 %collective-permute-done.37 = bf16[448,128]{1,0:T(8,128)(2,1)} collective-permute-done((bf16[448,128]{1,0:T(8,128)(2,1)S(1)}, bf16[448,128]{1,0:T(8,128)(2,1)}, u32[]{:S(2)}, u32[]{:S(2)}) %collective-permute-start.37) | collective-permute-done | bytes 114720 | tf_op jit(solution)/shard_map/ppermute | solution.py:216
  137.6 1.0 maximum_select_fusion.5
  138.7 1.6 collective-permute-start.38
  140.3 2.8 %collective-permute-start.27 = (bf16[448,128]{1,0:T(8,128)(2,1)S(1)}, bf16[448,128]{1,0:T(8,128)(2,1)S(1)}, u32[]{:S(2)}, u32[]{:S(2)}) collective-permute-start(bf16[448,128]{1,0:T(8,128)(2,1)S(1)} %maximum_select_fusion.6), channel_id=1, source_target_pairs={{0,4},{4,0},{8,12},{12,8},{16,20},{20,16},{24,28},{28,24},{1,5},{5... | collective-permute-start | bytes 344072 | tf_op jit(solution)/shard_map/ppermute | solution.py:216
  143.8 1.3 collective-permute-start.15
  145.1 1.3 collective-permute-start.16
  147.2 3.5 %collective-permute-start.28 = (bf16[896,128]{1,0:T(8,128)(2,1)}, bf16[896,128]{1,0:T(8,128)(2,1)}, u32[]{:S(2)}, u32[]{:S(2)}) collective-permute-start(bf16[896,128]{1,0:T(8,128)(2,1)} %maximum_select_fusion.4), channel_id=1, source_target_pairs={{0,2},{1,3},{2,0},{3,1},{4,6},{5,7},{6,4},{7,5},{8,10},{9,11},{10,... | collective-permute-start | bytes 688136 | tf_op jit(solution)/shard_map/ppermute | solution.py:216
  151.5 1.3 collective-permute-start.18
  153.5 1.3 collective-permute-start.19
  154.8 5.7 %collective-permute-done.19.yb = bf16[2,1,256,128]{3,2,1,0:T(8,128)(2,1)} collective-permute-done((bf16[2,1,256,128]{3,2,1,0:T(8,128)(2,1)}, bf16[2,1,256,128]{3,2,1,0:T(8,128)(2,1)}, u32[]{:S(2)}, u32[]{:S(2)}) %collective-permute-start.19) | collective-permute-done | bytes 131104 | tf_op jit(solution)/shard_map/ppermute | solution.py:190
  161.4 4.4 %shard_map.79 = bf16[2,4,256,128]{3,2,1,0:T(8,128)(2,1)} custom-call(bf16[2,4,256,128]{3,2,1,0:T(8,128)(2,1)S(1)} %shard_map.78.x.d, bf16[2,1,256,128]{3,2,1,0:T(8,128)(2,1)S(1)} %collective-permute-done.15.xt, bf16[2,1,256,128]{3,2,1,0:T(8,128)(2,1)S(1)} %copy-done.29, bf16[2,4,256,128]{3,2,1,0:T(8,128)(2,1)S(1)} %collective-permute-done.17.y, ...), custom_call_target="tpu_custom_call" | custom-call | tf_op jit(solution)/shard_map/pallas_call | solution.py:50
  165.8 1.4 maximum_select_fusion.2
  167.2 1.7 collective-permute-start.29
  169.0 1.7 maximum_select_fusion.1
  170.7 1.4 convert.7
  172.5 1.4 convert.5
  (125 shorter events, 15.8 us)
Async XLA Ops:
  0.6 22.1 %copy-start = (bf16[2,4,256,128]{3,2,1,0:T(8,128)(2,1)S(1)}, bf16[2,4,256,128]{3,2,1,0:T(8,128)(2,1)}, u32[]{:S(2)}) copy-start(bf16[2,4,256,128]{3,2,1,0:T(8,128)(2,1)} %x.3) | copy-start | bytes 1572868
  0.6 22.1 %collective-permute-start.2 = (bf16[2,4,256,128]{3,2,1,0:T(8,128)(2,1)}, bf16[2,4,256,128]{3,2,1,0:T(8,128)(2,1)S(1)}, u32[]{:S(2)}, u32[]{:S(2)}) collective-permute-start(bf16[2,4,256,128]{3,2,1,0:T(8,128)(2,1)} %x.3), channel_id=1, source_target_pairs={{0,4},{4,8},{8,12},{12,16},{16,20},{20,24},{24,28},{1,5},{5,9},{9,... | collective-permute-start | bytes 1572872 | tf_op jit(solution)/shard_map/ppermute | solution.py:186
  6.7 16.0 %collective-permute-start = (bf16[2,1,256,128]{3,2,1,0:T(8,128)(2,1)S(1)}, bf16[2,1,256,128]{3,2,1,0:T(8,128)(2,1)S(1)}, u32[]{:S(2)}, u32[]{:S(2)}) collective-permute-start(bf16[2,1,256,128]{3,2,1,0:T(8,128)(2,1)S(1)} %get-tuple-element.27), channel_id=1, source_target_pairs={{0,1},{1,2},{2,3},{4,5},{5,6},{6,7},{8,9},{9,10},{10,11},{12,13},{... | collective-permute-start | bytes 393224 | tf_op jit(solution)/shard_map/ppermute | solution.py:191
  8.2 14.5 %collective-permute-start.1 = (bf16[2,1,256,128]{3,2,1,0:T(8,128)(2,1)S(1)}, bf16[2,1,256,128]{3,2,1,0:T(8,128)(2,1)S(1)}, u32[]{:S(2)}, u32[]{:S(2)}) collective-permute-start(bf16[2,1,256,128]{3,2,1,0:T(8,128)(2,1)S(1)} %get-tuple-element.26), channel_id=1, source_target_pairs={{1,0},{2,1},{3,2},{5,4},{6,5},{7,6},{9,8},{10,9},{11,10},{13,12},{... | collective-permute-start | bytes 393224 | tf_op jit(solution)/shard_map/ppermute | solution.py:192
  9.5 13.2 %collective-permute-start.3 = (bf16[2,1,256,128]{3,2,1,0:T(8,128)(2,1)S(1)}, bf16[2,1,256,128]{3,2,1,0:T(8,128)(2,1)S(1)}, u32[]{:S(2)}, u32[]{:S(2)}) collective-permute-start(bf16[2,1,256,128]{3,2,1,0:T(8,128)(2,1)S(1)} %get-tuple-element.27), channel_id=1, source_target_pairs={{0,5},{1,6},{2,7},{4,9},{5,10},{6,11},{8,13},{9,14},{10,15},{12,17... | collective-permute-start | bytes 393224 | tf_op jit(solution)/shard_map/ppermute | solution.py:189
  15.2 7.5 %collective-permute-start.4 = (bf16[2,1,256,128]{3,2,1,0:T(8,128)(2,1)S(1)}, bf16[2,1,256,128]{3,2,1,0:T(8,128)(2,1)S(1)}, u32[]{:S(2)}, u32[]{:S(2)}) collective-permute-start(bf16[2,1,256,128]{3,2,1,0:T(8,128)(2,1)S(1)} %get-tuple-element.26), channel_id=1, source_target_pairs={{1,4},{2,5},{3,6},{5,8},{6,9},{7,10},{9,12},{10,13},{11,14},{13,16... | collective-permute-start | bytes 393224 | tf_op jit(solution)/shard_map/ppermute | solution.py:190
  15.9 1.2 copy-start.9
  17.0 1.2 copy-start.10
  19.8 1.4 copy-start.1
  21.2 1.4 copy-start.5
  22.6 3.0 %copy-start.3 = (bf16[12,384,256]{2,1,0:T(8,128)(2,1)}, bf16[12,384,256]{2,1,0:T(8,128)(2,1)S(1)}, u32[]{:S(2)}) copy-start(bf16[12,384,256]{2,1,0:T(8,128)(2,1)S(1)} %get-tuple-element.14.w) | copy-start | bytes 7077892
  22.6 3.0 %copy-start.12 = (bf16[2,1,256,128]{3,2,1,0:T(8,128)(2,1)}, bf16[2,1,256,128]{3,2,1,0:T(8,128)(2,1)S(1)}, u32[]{:S(2)}) copy-start(bf16[2,1,256,128]{3,2,1,0:T(8,128)(2,1)S(1)} %collective-permute-done.xt) | copy-start | bytes 393220
  22.7 3.0 %copy-start.14 = (bf16[2,1,256,128]{3,2,1,0:T(8,128)(2,1)}, bf16[2,1,256,128]{3,2,1,0:T(8,128)(2,1)S(1)}, u32[]{:S(2)}) copy-start(bf16[2,1,256,128]{3,2,1,0:T(8,128)(2,1)S(1)} %collective-permute-done.1.xb) | copy-start | bytes 393220
  22.7 3.0 %copy-start.16 = (bf16[2,1,256,128]{3,2,1,0:T(8,128)(2,1)}, bf16[2,1,256,128]{3,2,1,0:T(8,128)(2,1)S(1)}, u32[]{:S(2)}) copy-start(bf16[2,1,256,128]{3,2,1,0:T(8,128)(2,1)S(1)} %collective-permute-done.3.yt) | copy-start | bytes 393220
  22.7 3.0 %copy-start.18 = (bf16[2,1,256,128]{3,2,1,0:T(8,128)(2,1)}, bf16[2,1,256,128]{3,2,1,0:T(8,128)(2,1)S(1)}, u32[]{:S(2)}) copy-start(bf16[2,1,256,128]{3,2,1,0:T(8,128)(2,1)S(1)} %collective-permute-done.4.yb) | copy-start | bytes 393220
  22.7 23.4 %copy-start.11 = (bf16[2,4,256,128]{3,2,1,0:T(8,128)(2,1)S(1)}, bf16[2,4,256,128]{3,2,1,0:T(8,128)(2,1)}, u32[]{:S(2)}) copy-start(bf16[2,4,256,128]{3,2,1,0:T(8,128)(2,1)} %cot.1) | copy-start | bytes 1572868
  26.6 19.5 %collective-permute-start.7 = (bf16[2,4,256,128]{3,2,1,0:T(8,128)(2,1)S(1)}, bf16[2,4,256,128]{3,2,1,0:T(8,128)(2,1)S(1)}, u32[]{:S(2)}, u32[]{:S(2)}) collective-permute-start(bf16[2,4,256,128]{3,2,1,0:T(8,128)(2,1)S(1)} %get-tuple-element.13.x), channel_id=1, source_target_pairs={{0,4},{4,8},{8,12},{12,16},{16,20},{20,24},{24,28},{1,5},{5,9},{9,... | collective-permute-start | bytes 1572872 | tf_op jit(solution)/shard_map/ppermute | solution.py:186
  30.7 12.4 %collective-permute-start.5 = (bf16[2,1,256,128]{3,2,1,0:T(8,128)(2,1)S(1)}, bf16[2,1,256,128]{3,2,1,0:T(8,128)(2,1)S(1)}, u32[]{:S(2)}, u32[]{:S(2)}) collective-permute-start(bf16[2,1,256,128]{3,2,1,0:T(8,128)(2,1)S(1)} %get-tuple-element.25), channel_id=1, source_target_pairs={{0,1},{1,2},{2,3},{4,5},{5,6},{6,7},{8,9},{9,10},{10,11},{12,13},{... | collective-permute-start | bytes 393224 | tf_op jit(solution)/shard_map/ppermute | solution.py:191
  34.6 8.5 %collective-permute-start.6 = (bf16[2,1,256,128]{3,2,1,0:T(8,128)(2,1)S(1)}, bf16[2,1,256,128]{3,2,1,0:T(8,128)(2,1)S(1)}, u32[]{:S(2)}, u32[]{:S(2)}) collective-permute-start(bf16[2,1,256,128]{3,2,1,0:T(8,128)(2,1)S(1)} %get-tuple-element.24), channel_id=1, source_target_pairs={{1,0},{2,1},{3,2},{5,4},{6,5},{7,6},{9,8},{10,9},{11,10},{13,12},{... | collective-permute-start | bytes 393224 | tf_op jit(solution)/shard_map/ppermute | solution.py:192
  35.9 9.5 %collective-permute-start.8 = (bf16[2,1,256,128]{3,2,1,0:T(8,128)(2,1)S(1)}, bf16[2,1,256,128]{3,2,1,0:T(8,128)(2,1)S(1)}, u32[]{:S(2)}, u32[]{:S(2)}) collective-permute-start(bf16[2,1,256,128]{3,2,1,0:T(8,128)(2,1)S(1)} %get-tuple-element.25), channel_id=1, source_target_pairs={{0,5},{1,6},{2,7},{4,9},{5,10},{6,11},{8,13},{9,14},{10,15},{12,17... | collective-permute-start | bytes 393224 | tf_op jit(solution)/shard_map/ppermute | solution.py:189
  42.4 3.0 %collective-permute-start.9 = (bf16[2,1,256,128]{3,2,1,0:T(8,128)(2,1)S(1)}, bf16[2,1,256,128]{3,2,1,0:T(8,128)(2,1)S(1)}, u32[]{:S(2)}, u32[]{:S(2)}) collective-permute-start(bf16[2,1,256,128]{3,2,1,0:T(8,128)(2,1)S(1)} %get-tuple-element.24), channel_id=1, source_target_pairs={{1,4},{2,5},{3,6},{5,8},{6,9},{7,10},{9,12},{10,13},{11,14},{13,16... | collective-permute-start | bytes 393224 | tf_op jit(solution)/shard_map/ppermute | solution.py:190
  43.1 9.3 %copy-start.20 = (bf16[2,1,256,128]{3,2,1,0:T(8,128)(2,1)}, bf16[2,1,256,128]{3,2,1,0:T(8,128)(2,1)S(1)}, u32[]{:S(2)}) copy-start(bf16[2,1,256,128]{3,2,1,0:T(8,128)(2,1)S(1)} %collective-permute-done.5.xt) | copy-start | bytes 393220
  43.2 9.3 %copy-start.22 = (bf16[2,1,256,128]{3,2,1,0:T(8,128)(2,1)}, bf16[2,1,256,128]{3,2,1,0:T(8,128)(2,1)S(1)}, u32[]{:S(2)}) copy-start(bf16[2,1,256,128]{3,2,1,0:T(8,128)(2,1)S(1)} %collective-permute-done.6.xb) | copy-start | bytes 393220
  45.4 7.0 %copy-start.24 = (bf16[2,1,256,128]{3,2,1,0:T(8,128)(2,1)}, bf16[2,1,256,128]{3,2,1,0:T(8,128)(2,1)S(1)}, u32[]{:S(2)}) copy-start(bf16[2,1,256,128]{3,2,1,0:T(8,128)(2,1)S(1)} %collective-permute-done.8.yt) | copy-start | bytes 393220
  46.1 1.7 copy-start.4
  58.3 7.9 %collective-permute-start.30 = (bf16[1792,128]{1,0:T(8,128)(2,1)S(1)}, bf16[1792,128]{1,0:T(8,128)(2,1)}, u32[]{:S(2)}, u32[]{:S(2)}) collective-permute-start(bf16[1792,128]{1,0:T(8,128)(2,1)S(1)} %dynamic-slice_bitcast_fusion), channel_id=1, source_target_pairs={{0,1},{1,0},{2,3},{3,2},{4,5},{5,4},{6,7},{7,6},{8,9},{9,8},{10,11... | collective-permute-start | bytes 1376264 | tf_op jit(solution)/shard_map/ppermute | solution.py:211
  60.8 26.2 %copy-start.6 = (bf16[12,384,256]{2,1,0:T(8,128)(2,1)S(1)}, bf16[12,384,256]{2,1,0:T(8,128)(2,1)}, u32[]{:S(2)}) copy-start(bf16[12,384,256]{2,1,0:T(8,128)(2,1)} %copy-done.5) | copy-start | bytes 7077892
  60.8 8.8 %collective-permute-start.10 = (bf16[2,1,256,128]{3,2,1,0:T(8,128)(2,1)S(1)}, bf16[2,1,256,128]{3,2,1,0:T(8,128)(2,1)S(1)}, u32[]{:S(2)}, u32[]{:S(2)}) collective-permute-start(bf16[2,1,256,128]{3,2,1,0:T(8,128)(2,1)S(1)} %get-tuple-element.23), channel_id=1, source_target_pairs={{0,1},{1,2},{2,3},{4,5},{5,6},{6,7},{8,9},{9,10},{10,11},{12,13},{... | collective-permute-start | bytes 393224 | tf_op jit(solution)/shard_map/ppermute | solution.py:191
  62.9 12.8 %collective-permute-start.13 = (bf16[2,1,256,128]{3,2,1,0:T(8,128)(2,1)S(1)}, bf16[2,1,256,128]{3,2,1,0:T(8,128)(2,1)S(1)}, u32[]{:S(2)}, u32[]{:S(2)}) collective-permute-start(bf16[2,1,256,128]{3,2,1,0:T(8,128)(2,1)S(1)} %get-tuple-element.23), channel_id=1, source_target_pairs={{4,1},{5,2},{6,3},{8,5},{9,6},{10,7},{12,9},{13,10},{14,11},{16,13... | collective-permute-start | bytes 393224 | tf_op jit(solution)/shard_map/ppermute | solution.py:189
  63.6 12.1 %collective-permute-start.11 = (bf16[2,1,256,128]{3,2,1,0:T(8,128)(2,1)S(1)}, bf16[2,1,256,128]{3,2,1,0:T(8,128)(2,1)S(1)}, u32[]{:S(2)}, u32[]{:S(2)}) collective-permute-start(bf16[2,1,256,128]{3,2,1,0:T(8,128)(2,1)S(1)} %get-tuple-element.22), channel_id=1, source_target_pairs={{1,0},{2,1},{3,2},{5,4},{6,5},{7,6},{9,8},{10,9},{11,10},{13,12},{... | collective-permute-start | bytes 393224 | tf_op jit(solution)/shard_map/ppermute | solution.py:192
  64.9 11.9 %collective-permute-start.14 = (bf16[2,1,256,128]{3,2,1,0:T(8,128)(2,1)S(1)}, bf16[2,1,256,128]{3,2,1,0:T(8,128)(2,1)S(1)}, u32[]{:S(2)}, u32[]{:S(2)}) collective-permute-start(bf16[2,1,256,128]{3,2,1,0:T(8,128)(2,1)S(1)} %get-tuple-element.22), channel_id=1, source_target_pairs={{5,0},{6,1},{7,2},{9,4},{10,5},{11,6},{13,8},{14,9},{15,10},{17,12... | collective-permute-start | bytes 393224 | tf_op jit(solution)/shard_map/ppermute | solution.py:190
  66.2 20.8 %collective-permute-start.12 = (bf16[2,4,256,128]{3,2,1,0:T(8,128)(2,1)S(1)}, bf16[2,4,256,128]{3,2,1,0:T(8,128)(2,1)S(1)}, u32[]{:S(2)}, u32[]{:S(2)}) collective-permute-start(bf16[2,4,256,128]{3,2,1,0:T(8,128)(2,1)S(1)} %get-tuple-element.16.x.d), channel_id=1, source_target_pairs={{4,0},{8,4},{12,8},{16,12},{20,16},{24,20},{28,24},{5,1},{9,5},{13... | collective-permute-start | bytes 1572872 | tf_op jit(solution)/shard_map/ppermute | solution.py:186
  68.8 18.2 %copy-start.30 = (f32[1792,128]{1,0:T(8,128)}, f32[1792,128]{1,0:T(8,128)S(1)}, u32[]{:S(2)}) copy-start(f32[1792,128]{1,0:T(8,128)S(1)} %convert_add_fusion) | copy-start | bytes 2752516
  69.6 24.8 %collective-permute-start.31 = (bf16[896,128]{1,0:T(8,128)(2,1)}, bf16[896,128]{1,0:T(8,128)(2,1)}, u32[]{:S(2)}, u32[]{:S(2)}) collective-permute-start(bf16[896,128]{1,0:T(8,128)(2,1)} %fusion.1), channel_id=1, source_target_pairs={{0,2},{1,3},{2,0},{3,1},{4,6},{5,7},{6,4},{7,5},{8,10},{9,11},{10,... | collective-permute-start | bytes 688136 | tf_op jit(solution)/shard_map/ppermute | solution.py:211
  87.0 1.2 copy-start.8
  88.2 2.7 %copy-start.13 = (bf16[2,1,256,128]{3,2,1,0:T(8,128)(2,1)S(1)}, bf16[2,1,256,128]{3,2,1,0:T(8,128)(2,1)}, u32[]{:S(2)}) copy-start(bf16[2,1,256,128]{3,2,1,0:T(8,128)(2,1)} %copy-done.12) | copy-start | bytes 393220
  88.2 2.7 %copy-start.15 = (bf16[2,1,256,128]{3,2,1,0:T(8,128)(2,1)S(1)}, bf16[2,1,256,128]{3,2,1,0:T(8,128)(2,1)}, u32[]{:S(2)}) copy-start(bf16[2,1,256,128]{3,2,1,0:T(8,128)(2,1)} %copy-done.14) | copy-start | bytes 393220
  88.2 2.7 %copy-start.17 = (bf16[2,1,256,128]{3,2,1,0:T(8,128)(2,1)S(1)}, bf16[2,1,256,128]{3,2,1,0:T(8,128)(2,1)}, u32[]{:S(2)}) copy-start(bf16[2,1,256,128]{3,2,1,0:T(8,128)(2,1)} %copy-done.16) | copy-start | bytes 393220
  88.2 2.7 %copy-start.19 = (bf16[2,1,256,128]{3,2,1,0:T(8,128)(2,1)S(1)}, bf16[2,1,256,128]{3,2,1,0:T(8,128)(2,1)}, u32[]{:S(2)}) copy-start(bf16[2,1,256,128]{3,2,1,0:T(8,128)(2,1)} %copy-done.18) | copy-start | bytes 393220
  90.9 3.6 %copy-start.31 = (f32[1792,128]{1,0:T(8,128)S(1)}, f32[1792,128]{1,0:T(8,128)}, u32[]{:S(2)}) copy-start(f32[1792,128]{1,0:T(8,128)} %copy-done.30) | copy-start | bytes 2752516
  94.0 4.0 %collective-permute-start.20 = (bf16[1792,128]{1,0:T(8,128)(2,1)S(1)}, bf16[1792,128]{1,0:T(8,128)(2,1)S(1)}, u32[]{:S(2)}, u32[]{:S(2)}) collective-permute-start(bf16[1792,128]{1,0:T(8,128)(2,1)S(1)} %dynamic-slice_bitcast_fusion.1), channel_id=1, source_target_pairs={{0,1},{1,0},{2,3},{3,2},{4,5},{5,4},{6,7},{7,6},{8,9},{9,8},{10,11... | collective-permute-start | bytes 1376264 | tf_op jit(solution)/shard_map/ppermute | solution.py:211
  95.5 6.4 %collective-permute-start.32 = (bf16[448,128]{1,0:T(8,128)(2,1)S(1)}, bf16[448,128]{1,0:T(8,128)(2,1)S(1)}, u32[]{:S(2)}, u32[]{:S(2)}) collective-permute-start(bf16[448,128]{1,0:T(8,128)(2,1)S(1)} %fusion.3), channel_id=1, source_target_pairs={{0,4},{4,0},{8,12},{12,8},{16,20},{20,16},{24,28},{28,24},{1,5},{5... | collective-permute-start | bytes 344072 | tf_op jit(solution)/shard_map/ppermute | solution.py:211
  98.2 9.6 %collective-permute-start.21 = (bf16[896,128]{1,0:T(8,128)(2,1)S(1)}, bf16[896,128]{1,0:T(8,128)(2,1)S(1)}, u32[]{:S(2)}, u32[]{:S(2)}) collective-permute-start(bf16[896,128]{1,0:T(8,128)(2,1)S(1)} %fusion), channel_id=1, source_target_pairs={{0,2},{1,3},{2,0},{3,1},{4,6},{5,7},{6,4},{7,5},{8,10},{9,11},{10,... | collective-permute-start | bytes 688136 | tf_op jit(solution)/shard_map/ppermute | solution.py:211
  101.9 6.7 %collective-permute-start.33 = (bf16[224,128]{1,0:T(8,128)(2,1)S(1)}, bf16[224,128]{1,0:T(8,128)(2,1)S(1)}, u32[]{:S(2)}, u32[]{:S(2)}) collective-permute-start(bf16[224,128]{1,0:T(8,128)(2,1)S(1)} %fusion.5), channel_id=1, source_target_pairs={{0,8},{4,12},{8,0},{12,4},{16,24},{20,28},{24,16},{28,20},{1,9},{5... | collective-permute-start | bytes 172040 | tf_op jit(solution)/shard_map/ppermute | solution.py:211
  107.9 4.9 %collective-permute-start.22 = (bf16[448,128]{1,0:T(8,128)(2,1)S(1)}, bf16[448,128]{1,0:T(8,128)(2,1)S(1)}, u32[]{:S(2)}, u32[]{:S(2)}) collective-permute-start(bf16[448,128]{1,0:T(8,128)(2,1)S(1)} %fusion.2), channel_id=1, source_target_pairs={{0,4},{4,0},{8,12},{12,8},{16,20},{20,16},{24,28},{28,24},{1,5},{5... | collective-permute-start | bytes 344072 | tf_op jit(solution)/shard_map/ppermute | solution.py:211
  108.6 6.0 %collective-permute-start.34 = (bf16[112,128]{1,0:T(8,128)(2,1)S(1)}, bf16[112,128]{1,0:T(8,128)(2,1)S(1)}, u32[]{:S(2)}, u32[]{:S(2)}) collective-permute-start(bf16[112,128]{1,0:T(8,128)(2,1)S(1)} %fusion.9), channel_id=1, source_target_pairs={{0,16},{4,20},{8,24},{12,28},{16,0},{20,4},{24,8},{28,12},{1,17},{... | collective-permute-start | bytes 86024 | tf_op jit(solution)/shard_map/ppermute | solution.py:211
  112.8 47.7 %copy-start.2 = (bf16[12,384,256]{2,1,0:T(8,128)(2,1)S(1)}, bf16[12,384,256]{2,1,0:T(8,128)(2,1)}, u32[]{:S(2)}) copy-start(bf16[12,384,256]{2,1,0:T(8,128)(2,1)} %copy-done.1) | copy-start | bytes 7077892
  112.8 4.6 %collective-permute-start.23 = (bf16[224,128]{1,0:T(8,128)(2,1)S(1)}, bf16[224,128]{1,0:T(8,128)(2,1)S(1)}, u32[]{:S(2)}, u32[]{:S(2)}) collective-permute-start(bf16[224,128]{1,0:T(8,128)(2,1)S(1)} %fusion.4), channel_id=1, source_target_pairs={{0,8},{4,12},{8,0},{12,4},{16,24},{20,28},{24,16},{28,20},{1,9},{5... | collective-permute-start | bytes 172040 | tf_op jit(solution)/shard_map/ppermute | solution.py:211
  114.6 5.5 %collective-permute-start.35 = (bf16[112,128]{1,0:T(8,128)(2,1)S(1)}, bf16[112,128]{1,0:T(8,128)(2,1)S(1)}, u32[]{:S(2)}, u32[]{:S(2)}) collective-permute-start(bf16[112,128]{1,0:T(8,128)(2,1)S(1)} %fusion.6), channel_id=1, source_target_pairs={{0,16},{4,20},{8,24},{12,28},{16,0},{20,4},{24,8},{28,12},{1,17},{... | collective-permute-start | bytes 86024 | tf_op jit(solution)/shard_map/ppermute | solution.py:216
  117.4 4.9 %collective-permute-start.24 = (bf16[112,128]{1,0:T(8,128)(2,1)S(1)}, bf16[112,128]{1,0:T(8,128)(2,1)S(1)}, u32[]{:S(2)}, u32[]{:S(2)}) collective-permute-start(bf16[112,128]{1,0:T(8,128)(2,1)S(1)} %fusion.8), channel_id=1, source_target_pairs={{0,16},{4,20},{8,24},{12,28},{16,0},{20,4},{24,8},{28,12},{1,17},{... | collective-permute-start | bytes 86024 | tf_op jit(solution)/shard_map/ppermute | solution.py:211
  120.2 4.2 %collective-permute-start.36 = (bf16[224,128]{1,0:T(8,128)(2,1)S(1)}, bf16[224,128]{1,0:T(8,128)(2,1)S(1)}, u32[]{:S(2)}, u32[]{:S(2)}) collective-permute-start(bf16[224,128]{1,0:T(8,128)(2,1)S(1)} %maximum_select_fusion.9), channel_id=1, source_target_pairs={{0,8},{4,12},{8,0},{12,4},{16,24},{20,28},{24,16},{28,20},{1,9},{5... | collective-permute-start | bytes 172040 | tf_op jit(solution)/shard_map/ppermute | solution.py:216
  122.3 5.2 %collective-permute-start.25 = (bf16[112,128]{1,0:T(8,128)(2,1)S(1)}, bf16[112,128]{1,0:T(8,128)(2,1)}, u32[]{:S(2)}, u32[]{:S(2)}) collective-permute-start(bf16[112,128]{1,0:T(8,128)(2,1)S(1)} %fusion.7), channel_id=1, source_target_pairs={{0,16},{4,20},{8,24},{12,28},{16,0},{20,4},{24,8},{28,12},{1,17},{... | collective-permute-start | bytes 86024 | tf_op jit(solution)/shard_map/ppermute | solution.py:216
  124.5 13.2 %collective-permute-start.37 = (bf16[448,128]{1,0:T(8,128)(2,1)S(1)}, bf16[448,128]{1,0:T(8,128)(2,1)}, u32[]{:S(2)}, u32[]{:S(2)}) collective-permute-start(bf16[448,128]{1,0:T(8,128)(2,1)S(1)} %maximum_select_fusion.7), channel_id=1, source_target_pairs={{0,4},{4,0},{8,12},{12,8},{16,20},{20,16},{24,28},{28,24},{1,5},{5... | collective-permute-start | bytes 344072 | tf_op jit(solution)/shard_map/ppermute | solution.py:216
  124.6 35.9 %collective-permute-start.17 = (bf16[2,4,256,128]{3,2,1,0:T(8,128)(2,1)S(1)}, bf16[2,4,256,128]{3,2,1,0:T(8,128)(2,1)S(1)}, u32[]{:S(2)}, u32[]{:S(2)}) collective-permute-start(bf16[2,4,256,128]{3,2,1,0:T(8,128)(2,1)S(1)} %shard_map.78.x.d), channel_id=1, source_target_pairs={{4,0},{8,4},{12,8},{16,12},{20,16},{24,20},{28,24},{5,1},{9,5},{13... | collective-permute-start | bytes 1572872 | tf_op jit(solution)/shard_map/ppermute | solution.py:186
  128.4 11.9 %collective-permute-start.26 = (bf16[224,128]{1,0:T(8,128)(2,1)S(1)}, bf16[224,128]{1,0:T(8,128)(2,1)S(1)}, u32[]{:S(2)}, u32[]{:S(2)}) collective-permute-start(bf16[224,128]{1,0:T(8,128)(2,1)S(1)} %maximum_select_fusion.8), channel_id=1, source_target_pairs={{0,8},{4,12},{8,0},{12,4},{16,24},{20,28},{24,16},{28,20},{1,9},{5... | collective-permute-start | bytes 172040 | tf_op jit(solution)/shard_map/ppermute | solution.py:216
  138.7 12.0 %collective-permute-start.38 = (bf16[896,128]{1,0:T(8,128)(2,1)S(1)}, bf16[896,128]{1,0:T(8,128)(2,1)S(1)}, u32[]{:S(2)}, u32[]{:S(2)}) collective-permute-start(bf16[896,128]{1,0:T(8,128)(2,1)S(1)} %maximum_select_fusion.5), channel_id=1, source_target_pairs={{0,2},{1,3},{2,0},{3,1},{4,6},{5,7},{6,4},{7,5},{8,10},{9,11},{10,... | collective-permute-start | bytes 688136 | tf_op jit(solution)/shard_map/ppermute | solution.py:216
  140.3 6.1 %collective-permute-start.27 = (bf16[448,128]{1,0:T(8,128)(2,1)S(1)}, bf16[448,128]{1,0:T(8,128)(2,1)S(1)}, u32[]{:S(2)}, u32[]{:S(2)}) collective-permute-start(bf16[448,128]{1,0:T(8,128)(2,1)S(1)} %maximum_select_fusion.6), channel_id=1, source_target_pairs={{0,4},{4,0},{8,12},{12,8},{16,20},{20,16},{24,28},{28,24},{1,5},{5... | collective-permute-start | bytes 344072 | tf_op jit(solution)/shard_map/ppermute | solution.py:216
  143.8 7.7 %collective-permute-start.15 = (bf16[2,1,256,128]{3,2,1,0:T(8,128)(2,1)}, bf16[2,1,256,128]{3,2,1,0:T(8,128)(2,1)S(1)}, u32[]{:S(2)}, u32[]{:S(2)}) collective-permute-start(bf16[2,1,256,128]{3,2,1,0:T(8,128)(2,1)} %get-tuple-element.21), channel_id=1, source_target_pairs={{0,1},{1,2},{2,3},{4,5},{5,6},{6,7},{8,9},{9,10},{10,11},{12,13},{... | collective-permute-start | bytes 393224 | tf_op jit(solution)/shard_map/ppermute | solution.py:191
  145.1 7.8 %collective-permute-start.16 = (bf16[2,1,256,128]{3,2,1,0:T(8,128)(2,1)}, bf16[2,1,256,128]{3,2,1,0:T(8,128)(2,1)S(1)}, u32[]{:S(2)}, u32[]{:S(2)}) collective-permute-start(bf16[2,1,256,128]{3,2,1,0:T(8,128)(2,1)} %get-tuple-element.20), channel_id=1, source_target_pairs={{1,0},{2,1},{3,2},{5,4},{6,5},{7,6},{9,8},{10,9},{11,10},{13,12},{... | collective-permute-start | bytes 393224 | tf_op jit(solution)/shard_map/ppermute | solution.py:192
  147.2 18.7 %collective-permute-start.28 = (bf16[896,128]{1,0:T(8,128)(2,1)}, bf16[896,128]{1,0:T(8,128)(2,1)}, u32[]{:S(2)}, u32[]{:S(2)}) collective-permute-start(bf16[896,128]{1,0:T(8,128)(2,1)} %maximum_select_fusion.4), channel_id=1, source_target_pairs={{0,2},{1,3},{2,0},{3,1},{4,6},{5,7},{6,4},{7,5},{8,10},{9,11},{10,... | collective-permute-start | bytes 688136 | tf_op jit(solution)/shard_map/ppermute | solution.py:216
  151.5 17.4 %collective-permute-start.39 = (bf16[1792,128]{1,0:T(8,128)(2,1)}, bf16[1792,128]{1,0:T(8,128)(2,1)}, u32[]{:S(2)}, u32[]{:S(2)}) collective-permute-start(bf16[1792,128]{1,0:T(8,128)(2,1)} %maximum_select_fusion.3), channel_id=1, source_target_pairs={{0,1},{1,0},{2,3},{3,2},{4,5},{5,4},{6,7},{7,6},{8,9},{9,8},{10,11... | collective-permute-start | bytes 1376264 | tf_op jit(solution)/shard_map/ppermute | solution.py:216
  151.5 3.3 %collective-permute-start.18 = (bf16[2,1,256,128]{3,2,1,0:T(8,128)(2,1)}, bf16[2,1,256,128]{3,2,1,0:T(8,128)(2,1)}, u32[]{:S(2)}, u32[]{:S(2)}) collective-permute-start(bf16[2,1,256,128]{3,2,1,0:T(8,128)(2,1)} %get-tuple-element.21), channel_id=1, source_target_pairs={{4,1},{5,2},{6,3},{8,5},{9,6},{10,7},{12,9},{13,10},{14,11},{16,13... | collective-permute-start | bytes 393224 | tf_op jit(solution)/shard_map/ppermute | solution.py:189
  153.5 7.0 %collective-permute-start.19 = (bf16[2,1,256,128]{3,2,1,0:T(8,128)(2,1)}, bf16[2,1,256,128]{3,2,1,0:T(8,128)(2,1)}, u32[]{:S(2)}, u32[]{:S(2)}) collective-permute-start(bf16[2,1,256,128]{3,2,1,0:T(8,128)(2,1)} %get-tuple-element.20), channel_id=1, source_target_pairs={{5,0},{6,1},{7,2},{9,4},{10,5},{11,6},{13,8},{14,9},{15,10},{17,12... | collective-permute-start | bytes 393224 | tf_op jit(solution)/shard_map/ppermute | solution.py:190
  167.2 4.9 %collective-permute-start.29 = (bf16[1792,128]{1,0:T(8,128)(2,1)S(1)}, bf16[1792,128]{1,0:T(8,128)(2,1)S(1)}, u32[]{:S(2)}, u32[]{:S(2)}) collective-permute-start(bf16[1792,128]{1,0:T(8,128)(2,1)S(1)} %maximum_select_fusion.2), channel_id=1, source_target_pairs={{0,1},{1,0},{2,3},{3,2},{4,5},{5,4},{6,7},{7,6},{8,9},{9,8},{10,11... | collective-permute-start | bytes 1376264 | tf_op jit(solution)/shard_map/ppermute | solution.py:216
  (8 other events, 6.9 us)
